TPU v7x, 256 devices: a whole 4x4x8 slice. The times are simulated.
256 devices in a mesh: dp: 2 (over core), seq: 32 (over z, x), tensor: 4 (over y).
Axes of the slice: x: 4, y: 4, z: 8, core: 2. Of those that a mesh axis runs over, the one named last changes fastest.
Arguments:
- tokens: bfloat16 [2048, 4, 5120], P('seq', 'dp'), parts along dimension 1, may hold values from -6 to 6
- w_query: bfloat16 [5120, 5120], P(None, 'tensor'), may hold values from -0.5 to 0.5, as said below
- w_key: bfloat16 [5120, 5120], P(None, 'tensor'), may hold values from -0.5 to 0.5, as said below
- w_value: bfloat16 [5120, 5120], P(None, 'tensor'), may hold values from -0.078125 to 0.078125
- w_out: bfloat16 [5120, 5120], P('tensor'), may hold values from -0.125 to 0.125
- gain_query: float32 [5120], P('tensor'), may hold values from 0.5 to 4
- gain_key: float32 [5120], P('tensor'), may hold values from 0.5 to 4
Outputs:
- attended: bfloat16 [2048, 4, 5120], P(('seq', 'tensor'), 'dp'), parts along dimension 1
There are 2 independent parts, one for each index of `dp`. A program takes and returns all parts, laid end to end along the dimension named above; an argument that names none is the same for every part. Nothing has to cross between parts.
Inputs may be any that keep to these rules, and one draw needn't show every extreme that they name: `w_query`: entries of order 5120 ** -0.5 with unequal column scales. `w_key`: entries of order 5120 ** -0.5 with unequal column scales.
All inputs are finite; a program needn't handle non-finite values.
Results may differ from a plain program's by a relative error of at most 0.013.
The roundings to bfloat16 on the way count: a program that leaves them out, or rounds other values in their place, can miss the bound.
Values may be sent and summed in bfloat16 or wider, within the bound.
No kernel may reach another device: no remote copies, remote signals or barrier semaphores. Data moves between devices by JAX's collectives and lax.ppermute only.
A program may use at most 256 MiB of HBM per device.

v0:
```python
import jax
import jax.numpy as jnp
from jax import lax
from jax.sharding import PartitionSpec as P

HEADS = 40
HEAD_DIM = 128


def sent_to_all(array, axis):
    copies = jnp.broadcast_to(array, (lax.axis_size(axis), *array.shape))
    return lax.all_to_all(copies, axis, split_axis=0, concat_axis=0, tiled=True)


def of_everyone(array, axis):
    everything = sent_to_all(array, axis)
    return jnp.sum(everything, axis=0)


def together(arrays, axis):
    ravelled, at, outs = (jnp.concatenate([a.reshape(-1) for a in arrays]), 0, [])
    subtotal = of_everyone(ravelled, axis)
    for a in arrays:
        outs.append(subtotal[at : at + a.size].reshape(a.shape))
        at += a.size
    return tuple(outs)


def sent_together(arrays, axis, dim, along):
    ends, at = ([], 0)
    for a in arrays[:-1]:
        at += a.shape[along]
        ends.append(at)
    both = jnp.concatenate(arrays, axis=along)
    return tuple(jnp.split(lax.all_gather(both, axis, axis=dim, tiled=True), ends, axis=along))


def cut_along(array, dim, length):
    lengths = array.shape
    pieces = array.reshape(*lengths[:dim], length, lengths[dim] // length, *lengths[dim + 1 :])
    return jnp.moveaxis(pieces, dim, 0)


def summed_on_arrival(array, axis, dim):
    length = lax.axis_size(axis)
    pieces = lax.all_to_all(cut_along(array, dim, length), axis, 0, 0, tiled=True)
    return jnp.sum(pieces.astype(jnp.float32), axis=0)


def rotary(field, positions):
    half = HEAD_DIM // 2
    shaped = field.reshape(field.shape[0], -1, HEAD_DIM)
    freqs = jnp.exp(-jnp.log(500000.0) * jnp.arange(half, dtype=jnp.float32) * 2.0 / HEAD_DIM)
    angle = positions.astype(jnp.float32)[:, None] * freqs[None, :]
    cosine = jnp.cos(angle)[:, None, :]
    sine = jnp.sin(angle)[:, None, :]
    first = shaped[..., :half]
    second = shaped[..., half:]
    turned = jnp.concatenate(
        [first * cosine - second * sine, second * cosine + first * sine], axis=-1
    )
    return turned.reshape(field.shape[0], -1)


def local(tokens, w_query, w_key, w_value, w_out, gain_query, gain_key):
    tok_rows = tokens.shape[0]
    seq_count = tokens.shape[1]
    local_width = w_query.shape[1]
    local_heads = local_width // HEAD_DIM
    width = HEADS * HEAD_DIM
    flat = tokens.reshape(tok_rows * seq_count, tokens.shape[2])
    query = jnp.dot(flat, w_query, preferred_element_type=jnp.float32)
    key_raw = jnp.dot(flat, w_key, preferred_element_type=jnp.float32)
    sum_query, sum_key = together(
        (jnp.sum(query * query, axis=1), jnp.sum(key_raw * key_raw, axis=1)), "tensor"
    )
    value = jnp.dot(flat, w_value, preferred_element_type=jnp.float32).astype(jnp.bfloat16)
    scale_q = lax.rsqrt(sum_query / width + 1e-06)
    scale_k = lax.rsqrt(sum_key / width + 1e-06)
    my_block = lax.axis_index("seq")
    positions = my_block * tok_rows + jnp.arange(tok_rows, dtype=jnp.int32)
    row_positions = (positions[:, None] + jnp.zeros((1, seq_count), jnp.int32)).reshape(-1)
    q_normed = rotary(query * scale_q[:, None] * gain_query[None, :], row_positions).astype(
        jnp.bfloat16
    )
    k_normed = rotary(key_raw * scale_k[:, None] * gain_key[None, :], row_positions).astype(
        jnp.bfloat16
    )
    q_heads = q_normed.reshape(tok_rows, seq_count, local_heads, HEAD_DIM)
    k_local = k_normed.reshape(tok_rows, seq_count, local_width)
    v_local = value.reshape(tok_rows, seq_count, local_width)
    factor = HEAD_DIM ** (-0.5)

    def update(carry, key_block, value_block, key_pos):
        count = key_block.shape[0]
        key_heads = key_block.reshape(count, seq_count, local_heads, HEAD_DIM)
        value_heads = value_block.reshape(count, seq_count, local_heads, HEAD_DIM)
        scores = (
            jnp.einsum("qshd,kshd->shqk", q_heads, key_heads, preferred_element_type=jnp.float32)
            * factor
        )
        allowed = (key_pos[None, None, None, :] <= positions[None, None, :, None]) & (
            key_pos[None, None, None, :] >= 0
        )
        old_max, old_total, old_acc = carry
        new_max = jnp.maximum(old_max, jnp.max(jnp.where(allowed, scores, -1e30), axis=3))
        expo = jnp.where(allowed, jnp.exp(scores - new_max[..., None]), 0.0)
        new_total = jnp.sum(expo, axis=3)
        added = jnp.einsum(
            "shqk,kshd->shqd",
            expo.astype(jnp.bfloat16),
            value_heads,
            preferred_element_type=jnp.float32,
        )
        return (new_max, new_total, added)

    start_state = (
        jnp.full((seq_count, local_heads, tok_rows), -1e30, jnp.float32),
        jnp.zeros((seq_count, local_heads, tok_rows), jnp.float32),
        jnp.zeros((seq_count, local_heads, tok_rows, HEAD_DIM), jnp.float32),
    )
    piece = sent_together((k_local, v_local), "seq", 0, 1)
    key_pos = jnp.arange(piece[0].shape[0], dtype=jnp.int32)
    final_state = lax.cond(
        jnp.int32(0) > positions[tok_rows - 1],
        lambda state: state,
        lambda state: update(state, piece[0], piece[1], key_pos),
        start_state,
    )
    final_max, final_total, final_acc = final_state
    mixed = (final_acc / final_total[..., None]).astype(jnp.bfloat16)
    mixed = jnp.transpose(mixed, (2, 0, 1, 3)).reshape(tok_rows, seq_count, local_width)
    return summed_on_arrival(
        jnp.dot(mixed, w_out, preferred_element_type=jnp.float32).astype(jnp.bfloat16), "tensor", 0
    ).astype(jnp.bfloat16)


def solution(mesh):
    return jax.shard_map(
        local,
        mesh=mesh,
        in_specs=(
            P("seq", "dp", None),
            P(None, "tensor"),
            P(None, "tensor"),
            P(None, "tensor"),
            P("tensor", None),
            P("tensor"),
            P("tensor"),
        ),
        out_specs=P(("seq", "tensor"), "dp", None),
        check_vma=False,
    )
```

profile of v0, /device:TPU:8, one launch (start us, length us, event | category | flops | bytes accessed | tf_op | source)
XLA Modules:
  0.0 314.6 jit_solution(5106080428587252340)
XLA Ops:
  6.5 3.1 reshape.164
  9.7 6.8 %multiply_reduce_fusion.1 = (f32[128]{0:T(128)S(1)}, f32[128,1280]{1,0:T(8,128)S(1)}) fusion(bf16[128,5120]{1,0:T(8,128)(2,1)S(1)} %reshape.164, bf16[5120,1280]{1,0:T(8,128)(2,1)} %param.10), kind=kOutput, calls=%fused_computation.26 | convolution fusion | flops 1678049152 | bytes 15073792 | tf_op jit(solution)/shard_map/dot_general | solution.py:72
  16.5 1.6 copy-done
  18.1 2.0 multiply_reduce_fusion
  20.1 0.6 broadcast_in_dim.26
  20.7 5.3 %all-to-all-start = ((f32[4,1,256]{2,1,0:T(1,128)}), f32[4,1,256]{2,1,0:T(1,128)S(1)}, u32[]{:S(2)}, u32[]{:S(2)}) async-start(f32[4,1,256]{2,1,0:T(1,128)} %broadcast_in_dim.26), calls=%async_computation | async-start | bytes 8192 | tf_op jit(solution)/shard_map/all_to_all | solution.py:12
  26.1 0.1 convert_element_type.48
  26.3 6.6 %convolution_convert_fusion = bf16[128,1280]{1,0:T(8,128)(2,1)S(1)} fusion(bf16[128,5120]{1,0:T(8,128)(2,1)S(1)} %reshape.164, bf16[5120,1280]{1,0:T(8,128)(2,1)} %param.12), kind=kOutput, calls=%fused_computation.19 | convolution fusion | flops 1677885440 | bytes 14745600 | tf_op jit(solution)/shard_map/dot_general | solution.py:77
  32.9 0.2 multiply_cosine_fusion
  33.1 0.8 reshape.167
  34.0 0.2 multiply_multiply_fusion
  34.2 0.2 copy.47
  34.4 0.1 subtract_convert_fusion
  34.6 0.4 copy.48
  35.0 0.2 convert_element_type.49
  35.2 2.5 pad_maximum_fusion.1
  37.7 0.6 slice.21
  39.0 0.2 copy.46
  39.2 0.1 multiply_subtract_fusion
  39.3 161.9 %all-gather.2.cloned.1.call-done = bf16[2048,4,1280]{2,1,0:T(4,128)(2,1)} async-done(((bf16[64,4,1280]{2,1,0:T(4,128)(2,1)}), bf16[2048,4,1280]{2,1,0:T(4,128)(2,1)}) %all-gather.2.cloned.1.call-update) | async-done | bytes 20971536 | tf_op jit(solution)/shard_map/all_gather | solution.py:35
  201.2 78.1 %conditional.1 = (f32[2,10,64]{2,1,0:T(8,128)S(1)}, f32[2,10,64,128]{3,2,1,0:T(8,128)S(1)}) conditional(s32[]{:T(128)} %bitcast.3, (s32[2048]{0:T(1024)S(1)}, s32[64]{0:T(128)S(1)}, s32[2048]{0:T(1024)S(1)}, bf16[128,10,128]{0,2,1:T(8,128)(2,1)S(1)}, bf16[2048,4,1280]{2,1,0:T(4,128)(2,1)}) %tuple.13, () %tuple.14), branch_computations={%region_3.6_spmd, %region_6.7_spmd} | conditional | flops 1371276032 | bytes 138529040 | solution.py:124
  201.2 32.5 %copy.50 = bf16[2048,4,1280]{0,2,1:T(8,128)(2,1)} copy(bf16[2048,4,1280]{2,1,0:T(4,128)(2,1)} %get-tuple-element.47) | data formatting | bytes 41943040 | tf_op jit(solution)/shard_map
  233.7 16.5 %fusion.21 = (bf16[2048,2,1280]{0,2,1:T(8,128)(2,1)}, bf16[2048,2,1280]{0,2,1:T(8,128)(2,1)}) fusion(bf16[2048,4,1280]{0,2,1:T(8,128)(2,1)} %copy.50), kind=kLoop, calls=%fused_computation.43 | loop fusion | bytes 41943040 | tf_op jit(solution)/shard_map/split | solution.py:35
  250.2 0.2 compare_and_fusion
  250.3 0.4 copy.49
  250.8 11.2 %select_reduce_fusion = (f32[2,10,64]{2,1,0:T(8,128)S(1)}, f32[2,10,64,2048]{3,2,1,0:T(8,128)}) fusion(pred[64,2048]{1,0:T(8,128)(4,1)S(1)} %compare_and_fusion, bf16[2048,2,10,128]{0,3,2,1:T(8,128)(2,1)} %bitcast.28, bf16[64,2,10,128]{3,2,1,0:T(8,128)(2,1)S(1)} %bitcast.32), kind=kOutput, calls=%fused_computation.1 | convolution fusion | flops 678951680 | bytes 21435392 | tf_op jit(solution)/shard_map/cond/branch_0_fun/qshd,kshd->shqk/dot_general | solution.py:99
  261.9 10.8 %fusion.2 = f32[2,10,64,128]{3,2,1,0:T(8,128)S(1)} fusion(bf16[2048,2,10,128]{0,3,2,1:T(8,128)(2,1)} %bitcast.29, f32[2,10,64,2048]{3,2,1,0:T(8,128)} %get-tuple-element.51, f32[2,10,64]{2,1,0:T(8,128)S(1)} %broadcast_maximum_fusion, pred[64,2048]{1,0:T(8,128)(4,1)S(1)} %compare_and_fusion), kind=kOutput, calls=%fused_computation.4 | convolution fusion | flops 681574400 | bytes 21763072 | tf_op jit(solution)/shard_map/cond/branch_0_fun/shqk,kshd->shqd/dot_general | solution.py:109
  272.7 6.5 %fusion.1 = f32[2,10,64]{2,1,0:T(8,128)S(1)} fusion(f32[2,10,64,2048]{3,2,1,0:T(8,128)} %get-tuple-element.51, f32[2,10,64]{2,1,0:T(8,128)S(1)} %broadcast_maximum_fusion, pred[64,2048]{1,0:T(8,128)(4,1)S(1)} %compare_and_fusion), kind=kLoop, calls=%fused_computation.3 | loop fusion | flops 10484480 | bytes 10627072 | tf_op jit(solution)/shard_map/cond/branch_0_fun/reduce_sum | solution.py:108
  279.3 6.6 %fusion.14 = bf16[64,2,5120]{2,0,1:T(8,128)(2,1)S(1)} fusion(bf16[1280,5120]{1,0:T(8,128)(2,1)} %param.13, f32[2,10,64,128]{3,2,1,0:T(8,128)S(1)} %get-tuple-element.26, f32[2,10,64]{2,1,0:T(8,128)S(1)} %get-tuple-element.27), kind=kOutput, calls=%fused_computation.18 | convolution fusion | flops 1678704640 | bytes 15078400 | tf_op jit(solution)/shard_map/dot_general | solution.py:134
  286.0 20.3 %all_to_all.11 = bf16[4,16,2,5120]{3,1,2,0:T(8,128)(2,1)S(1)} all-to-all(bf16[4,16,2,5120]{3,1,2,0:T(8,128)(2,1)S(1)} %copy.52), channel_id=1, replica_groups=mesh['dp'=2,'seq'=32,'tensor'=4] {'tensor'}, dimensions={0} | all-to-all | bytes 2621440 | tf_op jit(solution)/shard_map/all_to_all | solution.py:46
  306.4 0.3 reduce_sum.51
  306.7 1.1 copy.54
  (21 shorter events, 0.3 us)
Async XLA Ops:
  9.7 8.5 %copy-start = (bf16[5120,1280]{1,0:T(8,128)(2,1)S(1)}, bf16[5120,1280]{1,0:T(8,128)(2,1)}, u32[]{:S(2)}) copy-start(bf16[5120,1280]{1,0:T(8,128)(2,1)} %param.11) | copy-start | bytes 39321604
  20.7 13.3 %all-to-all-start = ((f32[4,1,256]{2,1,0:T(1,128)}), f32[4,1,256]{2,1,0:T(1,128)S(1)}, u32[]{:S(2)}, u32[]{:S(2)}) async-start(f32[4,1,256]{2,1,0:T(1,128)} %broadcast_in_dim.26), calls=%async_computation | async-start | bytes 8192 | tf_op jit(solution)/shard_map/all_to_all | solution.py:12
  26.0 175.2 %all-gather.2.cloned.1.call-start = ((), (), s32[]{:S(2)}) async-start(), calls=%async_computation.2 | async-start | bytes 21626880 | tf_op jit(solution)/shard_map/all_gather | solution.py:35
  26.3 7.7 %copy-start.1 = (f32[1280]{0:T(1024)S(1)}, f32[1280]{0:T(1024)}, u32[]{:S(2)}) copy-start(f32[1280]{0:T(1024)} %param.15) | copy-start | bytes 15364
  26.3 7.7 %copy-start.2 = (f32[1280]{0:T(1024)S(1)}, f32[1280]{0:T(1024)}, u32[]{:S(2)}) copy-start(f32[1280]{0:T(1024)} %param.14) | copy-start | bytes 15364
Sparse Core Ops, SparseCore 0:
  37.8 163.3 all-gather.1
where the time goes:
time: 316 us; the launch traced here: 315 us
  waiting for transfers between devices  162 us (51%)
  local copies, waits for them, and re-layouts  58.5 us (19%)
  matrix products  44 us (14%)
  blocking collectives  20.3 us (6%)
  between operations  14.2 us (4%)
  other arithmetic  10.2 us (3%)
  starting transfers between devices  5.34 us (2%)
    all_gather x1, waiting for transfers between devices, sent_together(): lax.all_gather(both, axis, axis=dim, tiled=True)  162 us
    another operation x2, local copies, waits for them, and re-layouts  32.9 us
    all_to_all x1, blocking collectives, summed_on_arrival(): lax.all_to_all(cut_along(array, dim, length), axis, 0, 0, tiled=True)  20.3 us
    split x1, local copies, waits for them, and re-layouts, sent_together(): jnp.split(lax.all_gather(both, axis, axis=dim, tiled=True), ends, axis=al...  16.5 us
    dot_general x1, matrix products, update(): jnp.einsum('qshd,kshd->shqk', q_heads, key_heads, preferred_element_type=...  11.2 us
    dot_general x1, matrix products, update(): jnp.einsum('shqk,kshd->shqd', expo.astype(jnp.bfloat16), value_heads, pre...  10.8 us
    dot_general x1, matrix products, local(): query = jnp.dot(flat, w_query, preferred_element_type=jnp.float32)  6.83 us
    dot_general x1, matrix products, local(): jnp.dot(mixed, w_out, preferred_element_type=jnp.float32)  6.65 us
  transfers between devices with their start and end apart: 2, of which 1 were waited for; matrix products, arithmetic and copies ran while one was open for 3% of the time, Pallas kernels for 0%

commit v1 on v0

v1 whole, which is shorter than its diff:
```python
import jax
import jax.numpy as jnp
from jax import lax
from jax.experimental import pallas as pl
from jax.experimental.pallas import tpu as pltpu
from jax.sharding import PartitionSpec as P

HEADS = 40
HEAD_DIM = 128
HALF = HEAD_DIM // 2
LOG2E = 1.4426950408889634
BLOCK = 256


def turn_tables(first_token, rows):
    freqs = jnp.exp(-jnp.log(500000.0) * jnp.arange(HALF, dtype=jnp.float32) * 2.0 / HEAD_DIM)
    positions = first_token + jnp.arange(rows, dtype=jnp.int32)
    angle = positions.astype(jnp.float32)[:, None] * freqs[None, :]
    cosine, sine = jnp.cos(angle), jnp.sin(angle)
    return jnp.concatenate([cosine, cosine], 1), jnp.concatenate([-sine, sine], 1)


def pack_value(value, slots, seqs, rows, heads):
    def body(v_ref, out_ref, head_ref):
        for h in range(heads):
            head_ref[h] = v_ref[:, h * HEAD_DIM : (h + 1) * HEAD_DIM]
            for j in range(seqs):
                part = head_ref[h, pl.ds(j, rows, stride=seqs), :]
                out_ref[j * heads + h] = part.astype(jnp.bfloat16)

    return pl.pallas_call(
        body,
        out_shape=jax.ShapeDtypeStruct((slots, rows, HEAD_DIM), jnp.bfloat16),
        scratch_shapes=[pltpu.VMEM((heads, seqs * rows, HEAD_DIM), jnp.float32)],
        name="pack_value",
    )(value)


def pack_query_key(query, key, scale_q, scale_k, gain_q, gain_k, cosine, sine, slots, seqs, rows, heads):
    def body(q_ref, k_ref, sq_ref, sk_ref, gq_ref, gk_ref, c_ref, s_ref, out_ref, head_ref):
        cos, sin = c_ref[...], s_ref[...]
        for which, (x_ref, r_ref, g_ref) in enumerate(((q_ref, sq_ref, gq_ref), (k_ref, sk_ref, gk_ref))):
            for h in range(heads):
                cols = slice(h * HEAD_DIM, (h + 1) * HEAD_DIM)
                head_ref[which, h] = x_ref[:, cols] * r_ref[...] * g_ref[:, cols]
                for j in range(seqs):
                    part = head_ref[which, h, pl.ds(j, rows, stride=seqs), :]
                    turned = part * cos + pltpu.roll(part, HALF, 1) * sin
                    out_ref[j * heads + h, which] = turned.astype(jnp.bfloat16)

    return pl.pallas_call(
        body,
        out_shape=jax.ShapeDtypeStruct((slots, 2, rows, HEAD_DIM), jnp.bfloat16),
        scratch_shapes=[pltpu.VMEM((2, heads, seqs * rows, HEAD_DIM), jnp.float32)],
        name="pack_query_key",
    )(query, key, scale_q, scale_k, gain_q, gain_k, cosine, sine)


def attend(query_key, value):
    blocks, rows = value.shape[0], value.shape[1]
    per = BLOCK // rows
    steps = blocks // per
    power = HEAD_DIM ** (-0.5) * LOG2E

    def body(qk_ref, v_ref, out_ref, s_ref):
        row = lax.broadcasted_iota(jnp.int32, (BLOCK, BLOCK), 0)
        col = lax.broadcasted_iota(jnp.int32, (BLOCK, BLOCK), 1)
        for i in range(steps):
            q = qk_ref[per * i : per * (i + 1), 0].reshape(BLOCK, HEAD_DIM)
            top = None
            for c in range(i + 1):
                k = qk_ref[per * c : per * (c + 1), 1].reshape(BLOCK, HEAD_DIM)
                s = lax.dot_general(q, k, (((1,), (1,)), ((), ())), preferred_element_type=jnp.float32)
                if c == i:
                    s = jnp.where(col <= row, s, -1e30)
                s_ref[:, c * BLOCK : (c + 1) * BLOCK] = s
                best = jnp.maximum(s[:, :HEAD_DIM], s[:, HEAD_DIM:])
                top = best if top is None else jnp.maximum(top, best)
            top = jnp.max(top, axis=1, keepdims=True)
            total = jnp.zeros((BLOCK, HEAD_DIM), jnp.float32)
            acc = jnp.zeros((BLOCK, HEAD_DIM), jnp.float32)
            for c in range(i + 1):
                e = jnp.exp2((s_ref[:, c * BLOCK : (c + 1) * BLOCK] - top) * power)
                total = total + e[:, :HEAD_DIM] + e[:, HEAD_DIM:]
                v = v_ref[per * c : per * (c + 1)].reshape(BLOCK, HEAD_DIM)
                acc = acc + jnp.dot(e.astype(jnp.bfloat16), v, preferred_element_type=jnp.float32)
            mixed = acc / jnp.sum(total, axis=1, keepdims=True)
            out_ref[per * i : per * (i + 1)] = mixed.astype(jnp.bfloat16).reshape(per, rows, HEAD_DIM)

    return pl.pallas_call(
        body,
        out_shape=jax.ShapeDtypeStruct((blocks, rows, HEAD_DIM), jnp.bfloat16),
        scratch_shapes=[pltpu.VMEM((BLOCK, blocks * rows), jnp.float32)],
        name="attend",
    )(query_key, value)


def unpack_mixed(parts, seqs, heads):
    rows = parts.shape[1]

    def body(in_ref, out_ref, head_ref):
        for h in range(heads):
            for j in range(seqs):
                head_ref[h, pl.ds(j, rows, stride=seqs), :] = in_ref[j * heads + h].astype(jnp.float32)
            out_ref[:, h * HEAD_DIM : (h + 1) * HEAD_DIM] = head_ref[h].astype(jnp.bfloat16)

    return pl.pallas_call(
        body,
        out_shape=jax.ShapeDtypeStruct((rows * seqs, heads * HEAD_DIM), jnp.bfloat16),
        scratch_shapes=[pltpu.VMEM((heads, rows * seqs, HEAD_DIM), jnp.float32)],
        name="unpack_mixed",
    )(parts)


def exchange(array, axis):
    return lax.all_to_all(array, axis, 0, 0, tiled=True)


def local(tokens, w_query, w_key, w_value, w_out, gain_query, gain_key):
    rows, seqs, depth = tokens.shape
    local_width = w_query.shape[1]
    heads = local_width // HEAD_DIM
    width = HEADS * HEAD_DIM
    slots = lax.axis_size("seq")
    flat = tokens.reshape(rows * seqs, depth)
    cosine, sine = turn_tables(lax.axis_index("seq") * rows, rows)

    value = jnp.dot(flat, w_value, preferred_element_type=jnp.float32)
    sent_v = pack_value(value, slots, seqs, rows, heads)
    flat, sent_v = lax.optimization_barrier((flat, sent_v))
    got_v = exchange(sent_v, "seq")

    query = jnp.dot(flat, w_query, preferred_element_type=jnp.float32)
    key_raw = jnp.dot(flat, w_key, preferred_element_type=jnp.float32)
    squares = jnp.concatenate([jnp.sum(query * query, axis=1), jnp.sum(key_raw * key_raw, axis=1)])
    everyone = jnp.broadcast_to(squares, (lax.axis_size("tensor"), *squares.shape))
    sums = jnp.sum(exchange(everyone, "tensor"), axis=0)
    scales = lax.rsqrt(sums / width + 1e-06)
    lanes = jnp.broadcast_to(scales[:, None], (scales.shape[0], HEAD_DIM))
    sent_qk = pack_query_key(
        query, key_raw, lanes[: rows * seqs], lanes[rows * seqs :], gain_query[None, :], gain_key[None, :],
        cosine, sine, slots, seqs, rows, heads,
    )
    got_qk = exchange(sent_qk, "seq")

    mixed = exchange(attend(got_qk, got_v), "seq")
    flat_mixed = unpack_mixed(mixed[: seqs * heads], seqs, heads)
    partial = jnp.dot(flat_mixed, w_out, preferred_element_type=jnp.float32).astype(jnp.bfloat16)
    pieces = exchange(partial.reshape(lax.axis_size("tensor"), -1, depth), "tensor")
    attended = jnp.sum(pieces.astype(jnp.float32), axis=0).astype(jnp.bfloat16)
    return attended.reshape(-1, seqs, depth)


def solution(mesh):
    return jax.shard_map(
        local,
        mesh=mesh,
        in_specs=(
            P("seq", "dp", None),
            P(None, "tensor"),
            P(None, "tensor"),
            P(None, "tensor"),
            P("tensor", None),
            P("tensor"),
            P("tensor"),
        ),
        out_specs=P(("seq", "tensor"), "dp", None),
        check_vma=False,
    )
```

time: 316 us -> 153 us (0.48)
  waiting for transfers between devices: 162 us -> 10.1 us
  blocking collectives: 20.3 us -> 78.9 us
  local copies, waits for them, and re-layouts: 58.5 us -> 7.32 us
  matrix products: 44 us -> 29.1 us
  between operations: 14.2 us -> 0.07 us
  Pallas kernels: 0 us -> 13.2 us
  other arithmetic: 10.2 us -> 1.26 us
  starting transfers between devices: 5.34 us -> 11.3 us
    all_gather x1 -> x0, waiting for transfers between devices: 162 us -> none  [sent_together(): lax.all_gather(both, axis, axis=dim, tiled=True)]
    all_to_all x1 -> x4, blocking collectives: 20.3 us -> 78.9 us  [exchange(): return lax.all_to_all(array, axis, 0, 0, tiled=True)]
    another operation x2 -> x0, local copies, waits for them, and re-layouts: 32.9 us -> none
    dot_general x4 -> x2, matrix products: 35.2 us -> 14.2 us  [the longest x1 7.44 us: local(): value = jnp.dot(flat, w_value, preferred_element_type=jnp.float32)]
    split x1 -> x0, local copies, waits for them, and re-layouts: 16.5 us -> none  [sent_together(): jnp.split(lax.all_gather(both, axis, axis=dim, tiled=True), ends, axis=al...]
    pallas_call x0 -> x4, Pallas kernels: none -> 13.2 us  [the longest x1 6.7 us: attend(): pl.pallas_call(body, out_shape=jax.ShapeDtypeStruct((blocks, rows, HEAD_D...]
    all_to_all x1, waiting for transfers between devices: 0.01 us -> 10.1 us  [exchange(): return lax.all_to_all(array, axis, 0, 0, tiled=True)]
    reduce_sum x3 -> x2, other arithmetic: 6.86 us -> 0.32 us  [the longest x1 0.3 us: local(): attended = jnp.sum(pieces.astype(jnp.float32), axis=0).astype(jnp.bfloat16)]
  transfers between devices with their start and end apart: 2 -> 1, of which waited for: 1 -> 1; matrix products, arithmetic and copies ran while one was open for 3% -> 2% of each run, Pallas kernels for 0% -> 2%
where the time goes in v1:
time: 153 us; the launch traced here: 151 us
  blocking collectives  78.9 us (52%)
  matrix products  29.1 us (19%)
  Pallas kernels  13.2 us (9%)
  starting transfers between devices  11.3 us (7%)
  waiting for transfers between devices  10.1 us (7%)
  local copies, waits for them, and re-layouts  7.32 us (5%)
    all_to_all x4, blocking collectives, exchange(): return lax.all_to_all(array, axis, 0, 0, tiled=True)  78.9 us
    all_to_all x1, starting transfers between devices, exchange(): return lax.all_to_all(array, axis, 0, 0, tiled=True)  11.3 us
    all_to_all x1, waiting for transfers between devices, exchange(): return lax.all_to_all(array, axis, 0, 0, tiled=True)  10.1 us
    dot_general x1, matrix products, local(): query = jnp.dot(flat, w_query, preferred_element_type=jnp.float32)  7.48 us
    dot_general x1, matrix products, local(): key_raw = jnp.dot(flat, w_key, preferred_element_type=jnp.float32)  7.45 us
    dot_general x1, matrix products, local(): value = jnp.dot(flat, w_value, preferred_element_type=jnp.float32)  7.44 us
    dot_general x1, matrix products, local(): jnp.dot(flat_mixed, w_out, preferred_element_type=jnp.float32)  6.72 us
    pallas_call x1, Pallas kernels, attend(): pl.pallas_call(body, out_shape=jax.ShapeDtypeStruct((blocks, rows, HEAD_D...  6.7 us
  transfers between devices with their start and end apart: 1, of which 1 were waited for; matrix products, arithmetic and copies ran while one was open for 2% of the time, Pallas kernels for 2%

profile of v1, /device:TPU:8, one launch (start us, length us, event | category | flops | bytes accessed | tf_op | source)
XLA Modules:
  0.0 151.3 jit_solution(12321559990146121602)
XLA Ops:
  0.0 3.1 %reshape.47 = bf16[128,5120]{1,0:T(8,128)(2,1)S(1)} reshape(bf16[64,2,5120]{2,1,0:T(2,128)(2,1)} %param.7) | data formatting | bytes 2621440 | tf_op jit(solution)/shard_map/reshape | solution.py:125
  3.1 7.4 %fusion.2.v_ref = f32[128,1280]{1,0:T(8,128)} fusion(bf16[128,5120]{1,0:T(8,128)(2,1)S(1)} %reshape.47, bf16[5120,1280]{1,0:T(8,128)(2,1)} %param.10), kind=kOutput, calls=%fused_computation.13 | convolution fusion | flops 1677721600 | bytes 15073280 | tf_op jit(solution)/shard_map/dot_general | solution.py:128
  10.6 2.0 %pack_value.1 = bf16[32,64,128]{2,1,0:T(8,128)(2,1)} custom-call(f32[128,1280]{1,0:T(8,128)} %fusion.2.v_ref), custom_call_target="tpu_custom_call" | custom-call | tf_op jit(solution)/shard_map/pack_value/pallas_call | solution.py:31
  12.5 7.5 %multiply_reduce_fusion = (f32[128]{0:T(128)S(1)}, f32[128,1280]{1,0:T(8,128)}) fusion(bf16[128,5120]{1,0:T(8,128)(2,1)S(1)} %reshape.47, bf16[5120,1280]{1,0:T(8,128)(2,1)} %param.9), kind=kOutput, calls=%fused_computation.1 | convolution fusion | flops 1678049152 | bytes 15073792 | tf_op jit(solution)/shard_map/dot_general | solution.py:134
  20.0 0.0 copy-start.1
  20.0 0.0 copy-start.2
  20.0 7.5 %multiply_reduce_fusion.1 = (f32[128]{0:T(128)S(1)}, f32[128,1280]{1,0:T(8,128)}) fusion(bf16[128,5120]{1,0:T(8,128)(2,1)S(1)} %reshape.47, bf16[5120,1280]{1,0:T(8,128)(2,1)} %param.8), kind=kOutput, calls=%fused_computation.2 | convolution fusion | flops 1678049152 | bytes 15073792 | tf_op jit(solution)/shard_map/dot_general | solution.py:133
  27.5 8.5 %all_to_all.26 = f32[4,1,256]{2,1,0:T(1,128)S(1)} all-to-all(f32[4,1,256]{2,1,0:T(1,128)S(1)} %broadcast_in_dim.19), channel_id=1, replica_groups=mesh['dp'=2,'seq'=32,'tensor'=4] {'tensor'}, dimensions={0} | all-to-all | bytes 8192 | tf_op jit(solution)/shard_map/all_to_all | solution.py:116
  36.0 11.3 %all-to-all-start.2 = ((bf16[32,64,128]{2,1,0:T(8,128)(2,1)}), bf16[32,64,128]{2,1,0:T(8,128)(2,1)S(1)}, u32[]{:S(2)}, u32[]{:S(2)}) async-start(bf16[32,64,128]{2,1,0:T(8,128)(2,1)} %pack_value.1), calls=%async_computation.2 | async-start | bytes 1048576 | tf_op jit(solution)/shard_map/all_to_all | solution.py:116
  47.4 0.0 copy-done.1
  47.4 0.6 broadcast_in_dim.22.gq_ref
  48.0 0.0 copy-done.2
  48.0 0.6 broadcast_in_dim.23.gk_ref
  48.6 0.2 fusion
  48.8 0.7 pad_maximum_fusion
  49.5 0.7 broadcast_in_dim.20.sq_ref
  50.3 0.7 broadcast_in_dim.21.sk_ref
  51.0 2.7 %pack_query_key.1 = bf16[32,2,64,128]{3,2,1,0:T(8,128)(2,1)} custom-call(f32[128,1280]{1,0:T(8,128)} %get-tuple-element.17.q_ref, f32[128,1280]{1,0:T(8,128)} %get-tuple-element.15.k_ref, f32[128,128]{1,0:T(8,128)} %broadcast_in_dim.20.sq_ref, f32[128,128]{1,0:T(8,128)} %broadcast_in_dim.21.sk_ref, f32[1,1280]{1,0:T(1,128)} %broadcast_in_dim.22.gq_ref, ...), custom_call_target="tpu_custom_call" | custom-call | tf_op jit(solution)/shard_map/pack_query_key/pallas_call | solution.py:51
  53.7 10.1 %all-to-all-done.2.v_ref = bf16[32,64,128]{2,1,0:T(8,128)(2,1)S(1)} async-done(((bf16[32,64,128]{2,1,0:T(8,128)(2,1)}), bf16[32,64,128]{2,1,0:T(8,128)(2,1)S(1)}, u32[]{:S(2)}, u32[]{:S(2)}) %all-to-all-start.2) | async-done | bytes 524320 | tf_op jit(solution)/shard_map/all_to_all | solution.py:116
  63.8 0.0 copy-start
  63.8 31.2 %all_to_all.27.qk_ref = bf16[32,2,64,128]{3,2,1,0:T(8,128)(2,1)} all-to-all(bf16[32,2,64,128]{3,2,1,0:T(8,128)(2,1)} %pack_query_key.1), channel_id=1, replica_groups=mesh['dp'=2,'seq'=32,'tensor'=4] {'seq'}, dimensions={0} | all-to-all | bytes 2097152 | tf_op jit(solution)/shard_map/all_to_all | solution.py:116
  95.1 0.0 copy-done
  95.1 6.7 %attend.1 = bf16[32,64,128]{2,1,0:T(8,128)(2,1)} custom-call(bf16[32,2,64,128]{3,2,1,0:T(8,128)(2,1)} %all_to_all.27.qk_ref, bf16[32,64,128]{2,1,0:T(8,128)(2,1)} %copy-done), custom_call_target="tpu_custom_call" | custom-call | tf_op jit(solution)/shard_map/attend/pallas_call | solution.py:90
  101.8 22.0 %all_to_all.28 = bf16[32,64,128]{2,1,0:T(8,128)(2,1)S(1)} all-to-all(bf16[32,64,128]{2,1,0:T(8,128)(2,1)} %attend.1), channel_id=1, replica_groups=mesh['dp'=2,'seq'=32,'tensor'=4] {'seq'}, dimensions={0} | all-to-all | bytes 1048576 | tf_op jit(solution)/shard_map/all_to_all | solution.py:116
  123.7 0.7 slice.18.in_ref
  124.5 1.8 %unpack_mixed.1 = bf16[128,1280]{1,0:T(8,128)(2,1)} custom-call(bf16[20,64,128]{2,1,0:T(8,128)(2,1)} %slice.18.in_ref), custom_call_target="tpu_custom_call" | custom-call | tf_op jit(solution)/shard_map/unpack_mixed/pallas_call | solution.py:107
  126.3 6.7 %convolution_convert_fusion = bf16[128,5120]{1,0:T(8,128)(2,1)S(1)} fusion(bf16[128,1280]{1,0:T(8,128)(2,1)} %unpack_mixed.1, bf16[1280,5120]{1,0:T(8,128)(2,1)} %param.11), kind=kOutput, calls=%fused_computation | convolution fusion | flops 1678376960 | bytes 14745600 | tf_op jit(solution)/shard_map/dot_general | solution.py:148
  133.0 17.1 %all_to_all.29 = bf16[4,32,5120]{2,1,0:T(8,128)(2,1)S(1)} all-to-all(bf16[4,32,5120]{2,1,0:T(8,128)(2,1)S(1)} %bitcast.9), channel_id=1, replica_groups=mesh['dp'=2,'seq'=32,'tensor'=4] {'tensor'}, dimensions={0} | all-to-all | bytes 2621440 | tf_op jit(solution)/shard_map/all_to_all | solution.py:116
  150.1 0.3 reduce_sum.42
  150.4 0.8 reshape.49
  (7 shorter events, 0.1 us)
Async XLA Ops:
  20.0 27.4 %copy-start.1 = (f32[1280]{0:T(1024)S(1)}, f32[1280]{0:T(1024)}, u32[]{:S(2)}) copy-start(f32[1280]{0:T(1024)} %param.12) | copy-start | bytes 15364
  20.0 28.0 %copy-start.2 = (f32[1280]{0:T(1024)S(1)}, f32[1280]{0:T(1024)}, u32[]{:S(2)}) copy-start(f32[1280]{0:T(1024)} %param.13) | copy-start | bytes 15364
  36.0 27.8 %all-to-all-start.2 = ((bf16[32,64,128]{2,1,0:T(8,128)(2,1)}), bf16[32,64,128]{2,1,0:T(8,128)(2,1)S(1)}, u32[]{:S(2)}, u32[]{:S(2)}) async-start(bf16[32,64,128]{2,1,0:T(8,128)(2,1)} %pack_value.1), calls=%async_computation.2 | async-start | bytes 1048576 | tf_op jit(solution)/shard_map/all_to_all | solution.py:116
  63.8 31.3 %copy-start = (bf16[32,64,128]{2,1,0:T(8,128)(2,1)}, bf16[32,64,128]{2,1,0:T(8,128)(2,1)S(1)}, u32[]{:S(2)}) copy-start(bf16[32,64,128]{2,1,0:T(8,128)(2,1)S(1)} %all-to-all-done.2.v_ref) | copy-start | bytes 1572868

commit v2 on v1

v2 whole, which is shorter than its diff:
```python
import jax
import jax.numpy as jnp
from jax import lax
from jax.experimental import pallas as pl
from jax.experimental.pallas import tpu as pltpu
from jax.sharding import PartitionSpec as P


HEADS = 40
HEAD_DIM = 128
HALF = HEAD_DIM // 2
LOG2E = 1.4426950408889634
BLOCK = 256
AHEAD = 4
ROWS_IN = 512


def row_of(column):
    return jnp.sum(column.T, axis=0, keepdims=True)


def stream(x_ref, weights, sums, buffer, arrived, before):
    block = buffer.shape[1]
    blocks = weights[0].shape[0] // block

    def copy(which, n):
        at = (which * blocks + n) % (AHEAD + 1)
        return pltpu.make_async_copy(weights[which].at[pl.ds(n * block, block), :], buffer.at[at], arrived.at[at])

    for n in range(AHEAD):
        copy(0, n).start()
    before()
    for which in range(len(weights)):

        def step(n, _, which=which):
            @pl.when(n + AHEAD < blocks)
            def _():
                copy(which, n + AHEAD).start()

            if which + 1 < len(weights):

                @pl.when(n + AHEAD >= blocks)
                def _():
                    copy(which + 1, n + AHEAD - blocks).start()

            copy(which, n).wait()
            columns = pl.ds(pl.multiple_of(n * block, block), block)
            part = buffer[(which * blocks + n) % (AHEAD + 1)]
            sums[which][...] += jnp.dot(x_ref[:, columns], part, preferred_element_type=jnp.float32)
            return 0

        sums[which][...] = jnp.zeros_like(sums[which])
        lax.fori_loop(0, blocks, step, 0)


def project_value(tokens, weight, slots):
    rows, seqs, depth = tokens.shape
    total, width = rows * seqs, weight.shape[1]
    heads = width // HEAD_DIM

    def body(in_ref, w_ref, x_ref, out_ref, sums, buffer, arrived, head_ref, token_ref, here):
        tokens_in = pltpu.make_async_copy(in_ref, token_ref, here)
        tokens_in.start()

        def before():
            tokens_in.wait()
            x_ref[...] = token_ref[...].reshape(total, depth)

        stream(x_ref, (w_ref,), (sums,), buffer, arrived, before)
        for h in range(heads):
            head_ref[h] = sums[:, h * HEAD_DIM : (h + 1) * HEAD_DIM]
            for j in range(seqs):
                out_ref[j * heads + h] = head_ref[h, pl.ds(j, rows, stride=seqs), :].astype(jnp.bfloat16)

    vmem = pl.BlockSpec(memory_space=pltpu.VMEM)
    return pl.pallas_call(
        body,
        in_specs=[pl.BlockSpec(memory_space=pltpu.HBM)] * 2,
        out_specs=[vmem, vmem],
        out_shape=[
            jax.ShapeDtypeStruct((total, depth), jnp.bfloat16),
            jax.ShapeDtypeStruct((slots, rows, HEAD_DIM), jnp.bfloat16),
        ],
        scratch_shapes=[
            pltpu.VMEM((total, width), jnp.float32),
            pltpu.VMEM((AHEAD + 1, ROWS_IN, width), jnp.bfloat16),
            pltpu.SemaphoreType.DMA((AHEAD + 1,)),
            pltpu.VMEM((heads, total, HEAD_DIM), jnp.float32),
            pltpu.VMEM(tokens.shape, jnp.bfloat16),
            pltpu.SemaphoreType.DMA,
        ],
        compiler_params=pltpu.CompilerParams(vmem_limit_bytes=53 << 20),
        name="project_value",
    )(tokens, weight)


def turn_tables(first_token, rows):
    def body(at_ref, c_ref, s_ref):
        lane = lax.broadcasted_iota(jnp.int32, (rows, HEAD_DIM), 1)
        token = at_ref[0] + lax.broadcasted_iota(jnp.int32, (rows, HEAD_DIM), 0)
        pair = jnp.where(lane < HALF, lane, lane - HALF).astype(jnp.float32)
        angle = token.astype(jnp.float32) * jnp.exp(-jnp.log(500000.0) * pair * 2.0 / HEAD_DIM)
        c_ref[...] = jnp.cos(angle)
        s_ref[...] = jnp.where(lane < HALF, -jnp.sin(angle), jnp.sin(angle))

    return pl.pallas_call(
        body,
        in_specs=[pl.BlockSpec(memory_space=pltpu.SMEM)],
        out_shape=[jax.ShapeDtypeStruct((rows, HEAD_DIM), jnp.float32)] * 2,
        compiler_params=pltpu.CompilerParams(vmem_limit_bytes=4 << 20),
        name="turn_tables",
    )(first_token)


def project_query_key(flat, w_query, w_key):
    total, _ = flat.shape
    heads = w_query.shape[1] // HEAD_DIM

    def body(x_ref, wq_ref, wk_ref, q_ref, k_ref, sums_ref, sums, buffer, arrived):
        stream(x_ref, (wq_ref, wk_ref), (sums.at[0], sums.at[1]), buffer, arrived, lambda: None)
        squares = []
        for which, out_ref in enumerate((q_ref, k_ref)):
            square = jnp.zeros((total, HEAD_DIM), jnp.float32)
            for h in range(heads):
                part = sums[which, :, h * HEAD_DIM : (h + 1) * HEAD_DIM]
                out_ref[h] = part
                square = square + part * part
            squares.append(row_of(square))
        sums_ref[...] = jnp.concatenate(squares * 4, axis=0)

    vmem, hbm = pl.BlockSpec(memory_space=pltpu.VMEM), pl.BlockSpec(memory_space=pltpu.HBM)
    return pl.pallas_call(
        body,
        in_specs=[vmem, hbm, hbm],
        out_specs=[vmem] * 3,
        out_shape=[
            jax.ShapeDtypeStruct((heads, total, HEAD_DIM), jnp.float32),
            jax.ShapeDtypeStruct((heads, total, HEAD_DIM), jnp.float32),
            jax.ShapeDtypeStruct((8, total), jnp.float32),
        ],
        scratch_shapes=[
            pltpu.VMEM((2, total, heads * HEAD_DIM), jnp.float32),
            pltpu.VMEM((AHEAD + 1, ROWS_IN, heads * HEAD_DIM), jnp.bfloat16),
            pltpu.SemaphoreType.DMA((AHEAD + 1,)),
        ],
        compiler_params=pltpu.CompilerParams(vmem_limit_bytes=53 << 20),
        name="project_query_key",
    )(flat, w_query, w_key)


def pack(query, key, sums, gains, cosine, sine, slots, seqs):
    heads, total, _ = query.shape
    rows, width = total // seqs, HEADS * HEAD_DIM

    def body(q_ref, k_ref, sums_ref, g_ref, c_ref, s_ref, out_ref, row_ref, head_ref):
        cos, sin = c_ref[...], s_ref[...]
        everyone = sums_ref[0]
        for other in range(1, sums_ref.shape[0]):
            everyone = everyone + sums_ref[other]
        scale = lax.rsqrt(everyone / width + 1e-06)
        for which, x_ref in enumerate((q_ref, k_ref)):
            row_ref[...] = jnp.broadcast_to(scale[which : which + 1, :], (HEAD_DIM, total)).T
            for h in range(heads):
                head_ref[h] = x_ref[h] * row_ref[...] * g_ref[which, h : h + 1, :]
                for j in range(seqs):
                    part = head_ref[h, pl.ds(j, rows, stride=seqs), :]
                    turned = part * cos + pltpu.roll(part, HALF, 1) * sin
                    out_ref[j * heads + h, which] = turned.astype(jnp.bfloat16)

    return pl.pallas_call(
        body,
        out_shape=jax.ShapeDtypeStruct((slots, 2, rows, HEAD_DIM), jnp.bfloat16),
        scratch_shapes=[
            pltpu.VMEM((total, HEAD_DIM), jnp.float32),
            pltpu.VMEM((heads, total, HEAD_DIM), jnp.float32),
        ],
        compiler_params=pltpu.CompilerParams(vmem_limit_bytes=16 << 20),
        name="pack",
    )(query, key, sums, gains, cosine, sine)


def attend(query_key, value):
    blocks, rows, _ = value.shape
    per = BLOCK // rows
    steps = blocks // per
    power = HEAD_DIM ** (-0.5) * LOG2E

    def body(in_ref, v_ref, out_ref, s_ref):
        row = lax.broadcasted_iota(jnp.int32, (BLOCK, BLOCK), 0)
        col = lax.broadcasted_iota(jnp.int32, (BLOCK, BLOCK), 1)
        for i in range(steps):
            q = in_ref[per * i : per * (i + 1), 0].reshape(BLOCK, HEAD_DIM)
            top = None
            for c in range(i + 1):
                k = in_ref[per * c : per * (c + 1), 1].reshape(BLOCK, HEAD_DIM)
                s = lax.dot_general(q, k, (((1,), (1,)), ((), ())), preferred_element_type=jnp.float32)
                if c == i:
                    s = jnp.where(col <= row, s, -1e30)
                s_ref[:, c * BLOCK : (c + 1) * BLOCK] = s
                best = jnp.maximum(s[:, :HEAD_DIM], s[:, HEAD_DIM:])
                top = best if top is None else jnp.maximum(top, best)
            top = jnp.max(top, axis=1, keepdims=True)
            total = jnp.zeros((BLOCK, HEAD_DIM), jnp.float32)
            acc = jnp.zeros((BLOCK, HEAD_DIM), jnp.float32)
            for c in range(i + 1):
                e = jnp.exp2((s_ref[:, c * BLOCK : (c + 1) * BLOCK] - top) * power)
                total = total + e[:, :HEAD_DIM] + e[:, HEAD_DIM:]
                v = v_ref[per * c : per * (c + 1)].reshape(BLOCK, HEAD_DIM)
                acc = acc + jnp.dot(e.astype(jnp.bfloat16), v, preferred_element_type=jnp.float32)
            mixed = acc / jnp.sum(total, axis=1, keepdims=True)
            out_ref[per * i : per * (i + 1)] = mixed.astype(jnp.bfloat16).reshape(per, rows, HEAD_DIM)

    return pl.pallas_call(
        body,
        out_shape=jax.ShapeDtypeStruct((blocks, rows, HEAD_DIM), jnp.bfloat16),
        scratch_shapes=[pltpu.VMEM((BLOCK, blocks * rows), jnp.float32)],
        compiler_params=pltpu.CompilerParams(vmem_limit_bytes=16 << 20),
        cost_estimate=pl.CostEstimate(
            flops=64 * (blocks * rows) ** 2 * HEAD_DIM,
            transcendentals=(blocks * rows) ** 2 // 2,
            bytes_accessed=8 * blocks * rows * HEAD_DIM,
        ),
        name="attend",
    )(query_key, value)


def project_out(parts, weight, seqs):
    rows = parts.shape[1]
    local_width, depth = weight.shape
    heads = local_width // HEAD_DIM
    wide = 512

    def body(in_ref, w_ref, out_ref, head_ref, x_ref):
        for h in range(heads):
            for j in range(seqs):
                head_ref[h, pl.ds(j, rows, stride=seqs), :] = in_ref[j * heads + h].astype(jnp.float32)
            x_ref[:, h * HEAD_DIM : (h + 1) * HEAD_DIM] = head_ref[h].astype(jnp.bfloat16)

        def step(n, _):
            columns = pl.ds(pl.multiple_of(n * wide, wide), wide)
            got = jnp.dot(x_ref[...], w_ref[:, columns], preferred_element_type=jnp.float32)
            out_ref[:, columns] = got.astype(jnp.bfloat16)
            return 0

        lax.fori_loop(0, depth // wide, step, 0)

    vmem = pl.BlockSpec(memory_space=pltpu.VMEM)
    return pl.pallas_call(
        body,
        in_specs=[vmem, vmem],
        out_specs=vmem,
        out_shape=jax.ShapeDtypeStruct((rows * seqs, depth), jnp.bfloat16),
        scratch_shapes=[
            pltpu.VMEM((heads, rows * seqs, HEAD_DIM), jnp.float32),
            pltpu.VMEM((rows * seqs, local_width), jnp.bfloat16),
        ],
        compiler_params=pltpu.CompilerParams(vmem_limit_bytes=8 << 20),
        cost_estimate=pl.CostEstimate(
            flops=2 * rows * seqs * local_width * depth, transcendentals=0, bytes_accessed=2 * local_width * depth
        ),
        name="project_out",
    )(parts, weight)


def exchange(array, axis):
    return lax.all_to_all(array, axis, 0, 0, tiled=True)


def local(tokens, w_query, w_key, w_value, w_out, gain_query, gain_key):
    rows, seqs, depth = tokens.shape
    heads = w_query.shape[1] // HEAD_DIM
    slots, fold = lax.axis_size("seq"), lax.axis_size("tensor")
    first_token = (lax.axis_index("seq") * rows).astype(jnp.int32)[None]
    gains = jnp.stack([gain_query, gain_key]).reshape(2, heads, HEAD_DIM)

    flat, sent_v = project_value(tokens, w_value, slots)
    got_v = exchange(sent_v, "seq")
    query, key_raw, squares = project_query_key(flat, w_query, w_key)
    cosine, sine = turn_tables(first_token, rows)
    others = [
        lax.ppermute(squares, "tensor", [(i, (i + shift) % fold) for i in range(fold)])
        for shift in range(1, fold)
    ]
    sent_qk = pack(query, key_raw, jnp.stack([squares, *others]), gains, cosine, sine, slots, seqs)
    mixed = exchange(attend(exchange(sent_qk, "seq"), got_v), "seq")
    partial = project_out(mixed, w_out, seqs)
    pieces = exchange(partial.reshape(fold, -1, depth), "tensor")
    attended = jnp.sum(pieces.astype(jnp.float32), axis=0).astype(jnp.bfloat16)
    return attended.reshape(-1, seqs, depth)


def solution(mesh):
    return jax.shard_map(
        local,
        mesh=mesh,
        in_specs=(
            P("seq", "dp", None),
            P(None, "tensor"),
            P(None, "tensor"),
            P(None, "tensor"),
            P("tensor", None),
            P("tensor"),
            P("tensor"),
        ),
        out_specs=P(("seq", "tensor"), "dp", None),
        check_vma=False,
    )
```

time: 153 us -> 124 us (0.81)
  matrix products: 29.1 us -> 0 us
  Pallas kernels: 13.2 us -> 28 us
  waiting for transfers between devices: 10.1 us -> 1.59 us
  local copies, waits for them, and re-layouts: 7.32 us -> 1.96 us
  starting transfers between devices: 11.3 us -> 16.3 us
  blocking collectives: 78.9 us -> 74.5 us
    dot_general x4 -> x0, matrix products: 29.1 us -> none  [the longest x1 7.48 us: local(): query = jnp.dot(flat, w_query, preferred_element_type=jnp.float32)]
    pallas_call x3 -> x5, Pallas kernels: 6.52 us -> 23.5 us  [the longest x1 11.6 us: project_query_key(): pl.pallas_call(body, in_specs=[vmem, hbm, hbm], out_specs=[vmem] * 3, out...]
    all_to_all x1, waiting for transfers between devices: 10.1 us -> 0.01 us  [exchange(): return lax.all_to_all(array, axis, 0, 0, tiled=True)]
    ppermute x0 -> x3, starting transfers between devices: none -> 5.01 us  [local(): lax.ppermute(squares, 'tensor', [(i, (i + shift) % fold) for i in range(f...]
    all_to_all x4 -> x3, blocking collectives: 78.9 us -> 74.5 us  [exchange(): return lax.all_to_all(array, axis, 0, 0, tiled=True)]
    reshape x1 -> x0, local copies, waits for them, and re-layouts: 3.11 us -> none  [local(): flat = tokens.reshape(rows * seqs, depth)]
    broadcast_in_dim x5 -> x0, local copies, waits for them, and re-layouts: 2.6 us -> none  [the longest x2 1.41 us: local(): lanes = jnp.broadcast_to(scales[:, None], (scales.shape[0], HEAD_DIM))]
    pallas_call x1, Pallas kernels: 6.7 us -> 4.54 us  [attend(): pl.pallas_call(body, out_shape=jax.ShapeDtypeStruct((blocks, rows, HEAD_D...]
  transfers between devices with their start and end apart: 1 -> 4, of which waited for: 1 -> 1; matrix products, arithmetic and copies ran while one was open for 2% -> 0% of each run, Pallas kernels for 2% -> 10%
where the time goes in v2:
time: 124 us; the launch traced here: 123 us
  blocking collectives  74.5 us (60%)
  Pallas kernels  28 us (23%)
  starting transfers between devices  16.3 us (13%)
  local copies, waits for them, and re-layouts  1.96 us (2%)
  waiting for transfers between devices  1.59 us (1%)
    all_to_all x3, blocking collectives, exchange(): return lax.all_to_all(array, axis, 0, 0, tiled=True)  74.5 us
    pallas_call x1, Pallas kernels, project_query_key(): pl.pallas_call(body, in_specs=[vmem, hbm, hbm], out_specs=[vmem] * 3, out...  11.6 us
    all_to_all x1, starting transfers between devices, exchange(): return lax.all_to_all(array, axis, 0, 0, tiled=True)  11.3 us
    pallas_call x1, Pallas kernels, project_value(): pl.pallas_call(body, in_specs=[pl.BlockSpec(memory_space=pltpu.HBM)] * 2,...  7.5 us
    ppermute x3, starting transfers between devices, local(): lax.ppermute(squares, 'tensor', [(i, (i + shift) % fold) for i in range(f...  5.01 us
    pallas_call x1, Pallas kernels, attend(): pl.pallas_call(body, out_shape=jax.ShapeDtypeStruct((blocks, rows, HEAD_D...  4.54 us
    pallas_call x1, Pallas kernels, project_out(): pl.pallas_call(body, in_specs=[vmem, vmem], out_specs=vmem, out_shape=jax...  3.65 us
  transfers between devices with their start and end apart: 4, of which 1 were waited for; matrix products, arithmetic and copies ran while one was open for 0% of the time, Pallas kernels for 10%

profile of v2, /device:TPU:8, one launch (start us, length us, event | category | flops | bytes accessed | tf_op | source)
XLA Modules:
  0.0 122.8 jit_solution(4686692928460813151)
XLA Ops:
  0.0 7.5 %project_value.1 = (bf16[128,5120]{1,0:T(8,128)(2,1)}, bf16[32,64,128]{2,1,0:T(8,128)(2,1)}) custom-call(bf16[64,2,5120]{2,1,0:T(2,128)(2,1)} %in_ref.1, bf16[5120,1280]{1,0:T(8,128)(2,1)} %w_ref.2), custom_call_target="tpu_custom_call" | custom-call | tf_op jit(solution)/shard_map/project_value/pallas_call | solution.py:76
  7.5 11.3 %all-to-all-start.1 = ((bf16[32,64,128]{2,1,0:T(8,128)(2,1)}), bf16[32,64,128]{2,1,0:T(8,128)(2,1)S(1)}, u32[]{:S(2)}, u32[]{:S(2)}) async-start(bf16[32,64,128]{2,1,0:T(8,128)(2,1)} %get-tuple-element.18), calls=%async_computation.1 | async-start | bytes 1048576 | tf_op jit(solution)/shard_map/all_to_all | solution.py:266
  18.8 0.0 copy-start.1
  18.9 0.0 copy-start.2
  18.9 11.6 %project_query_key.1 = (f32[10,128,128]{2,1,0:T(8,128)S(1)}, f32[10,128,128]{2,1,0:T(8,128)}, f32[8,128]{1,0:T(8,128)S(1)}) custom-call(bf16[128,5120]{1,0:T(8,128)(2,1)} %get-tuple-element.12.x_ref, bf16[5120,1280]{1,0:T(8,128)(2,1)} %wq_ref.1, bf16[5120,1280]{1,0:T(8,128)(2,1)} %wk_ref.1), custom_call_target="tpu_custom_call" | custom-call | tf_op jit(solution)/shard_map/project_query_key/pallas_call | solution.py:132
  30.4 1.7 %collective-permute-start = (f32[8,128]{1,0:T(8,128)S(1)}, f32[8,128]{1,0:T(8,128)S(1)}, u32[]{:S(2)}, u32[]{:S(2)}) collective-permute-start(f32[8,128]{1,0:T(8,128)S(1)} %get-tuple-element.15), channel_id=1, source_target_pairs={{0,1},{1,2},{2,3},{3,0},{4,5},{5,6},{6,7},{7,4},{8,9},{9,10},{10,1... | collective-permute-start | bytes 12296 | tf_op jit(solution)/shard_map/ppermute | solution.py:281
  32.1 0.9 collective-permute-start.1
  33.0 2.4 %collective-permute-start.2 = (f32[8,128]{1,0:T(8,128)S(1)}, f32[8,128]{1,0:T(8,128)S(1)}, u32[]{:S(2)}, u32[]{:S(2)}) collective-permute-start(f32[8,128]{1,0:T(8,128)S(1)} %get-tuple-element.15), channel_id=1, source_target_pairs={{0,3},{1,0},{2,1},{3,2},{4,7},{5,4},{6,5},{7,6},{8,11},{9,8},{10,9... | collective-permute-start | bytes 12296 | tf_op jit(solution)/shard_map/ppermute | solution.py:281
  35.4 0.0 copy-done.1
  35.4 0.0 copy-done.2
  35.5 0.1 turn_tables.1
  35.6 0.0 collective-permute-done
  35.6 1.6 %collective-permute-done.1 = f32[8,128]{1,0:T(8,128)S(1)} collective-permute-done((f32[8,128]{1,0:T(8,128)S(1)}, f32[8,128]{1,0:T(8,128)S(1)}, u32[]{:S(2)}, u32[]{:S(2)}) %collective-permute-start.1) | collective-permute-done | bytes 4128 | tf_op jit(solution)/shard_map/ppermute | solution.py:281
  37.2 0.0 collective-permute-done.2
  37.2 0.0 copy-start
  37.2 1.1 copy-done
  38.3 0.6 pack.1
  38.9 0.0 all-to-all-done.1.v_ref
  38.9 0.0 slice-start
  38.9 35.9 %all_to_all.20.in_ref = bf16[32,2,64,128]{3,2,1,0:T(8,128)(2,1)S(1)} all-to-all(bf16[32,2,64,128]{3,2,1,0:T(8,128)(2,1)S(1)} %pack.1), channel_id=1, replica_groups=mesh['dp'=2,'seq'=32,'tensor'=4] {'seq'}, dimensions={0} | all-to-all | bytes 2097152 | tf_op jit(solution)/shard_map/all_to_all | solution.py:266
  74.8 0.0 slice-start.1
  74.8 0.0 slice-start.2
  74.8 4.5 %attend.1 = bf16[32,64,128]{2,1,0:T(8,128)(2,1)S(1)} custom-call(bf16[32,2,64,128]{3,2,1,0:T(8,128)(2,1)S(1)} %all_to_all.20.in_ref, bf16[32,64,128]{2,1,0:T(8,128)(2,1)S(1)} %all-to-all-done.1.v_ref), custom_call_target="tpu_custom_call" | custom-call | flops 34359738368 | bytes 2097152 | tf_op jit(solution)/shard_map/attend/pallas_call | solution.py:213
  79.4 21.2 %all_to_all.21.in_ref = bf16[32,64,128]{2,1,0:T(8,128)(2,1)S(1)} all-to-all(bf16[32,64,128]{2,1,0:T(8,128)(2,1)S(1)} %attend.1), channel_id=1, replica_groups=mesh['dp'=2,'seq'=32,'tensor'=4] {'seq'}, dimensions={0} | all-to-all | bytes 1048576 | tf_op jit(solution)/shard_map/all_to_all | solution.py:266
  100.6 0.0 slice-done
  100.6 0.0 slice-done.1
  100.6 0.0 slice-done.2
  100.6 0.0 slice-done.3
  100.6 3.7 %project_out.1 = bf16[128,5120]{1,0:T(8,128)(2,1)S(1)} custom-call(bf16[32,64,128]{2,1,0:T(8,128)(2,1)S(1)} %all_to_all.21.in_ref, bf16[1280,5120]{1,0:T(8,128)(2,1)S(1)} %bitcast.9), custom_call_target="tpu_custom_call" | custom-call | flops 1677721600 | bytes 13107200 | tf_op jit(solution)/shard_map/project_out/pallas_call | solution.py:248
  104.3 17.4 %all_to_all.22 = bf16[4,32,5120]{2,1,0:T(8,128)(2,1)S(1)} all-to-all(bf16[4,32,5120]{2,1,0:T(8,128)(2,1)S(1)} %bitcast.10), channel_id=1, replica_groups=mesh['dp'=2,'seq'=32,'tensor'=4] {'tensor'}, dimensions={0} | all-to-all | bytes 2621440 | tf_op jit(solution)/shard_map/all_to_all | solution.py:266
  121.6 0.3 reduce_sum.12
  121.9 0.8 reshape.12
  (4 shorter events, 0.0 us)
Async XLA Ops:
  7.5 31.4 %all-to-all-start.1 = ((bf16[32,64,128]{2,1,0:T(8,128)(2,1)}), bf16[32,64,128]{2,1,0:T(8,128)(2,1)S(1)}, u32[]{:S(2)}, u32[]{:S(2)}) async-start(bf16[32,64,128]{2,1,0:T(8,128)(2,1)} %get-tuple-element.18), calls=%async_computation.1 | async-start | bytes 1048576 | tf_op jit(solution)/shard_map/all_to_all | solution.py:266
  18.8 16.6 %copy-start.1 = (f32[1280]{0:T(1024)S(1)}, f32[1280]{0:T(1024)}, u32[]{:S(2)}) copy-start(f32[1280]{0:T(1024)} %param.13) | copy-start | bytes 15364
  18.9 16.6 %copy-start.2 = (f32[1280]{0:T(1024)S(1)}, f32[1280]{0:T(1024)}, u32[]{:S(2)}) copy-start(f32[1280]{0:T(1024)} %param.12) | copy-start | bytes 15364
  30.4 5.2 %collective-permute-start = (f32[8,128]{1,0:T(8,128)S(1)}, f32[8,128]{1,0:T(8,128)S(1)}, u32[]{:S(2)}, u32[]{:S(2)}) collective-permute-start(f32[8,128]{1,0:T(8,128)S(1)} %get-tuple-element.15), channel_id=1, source_target_pairs={{0,1},{1,2},{2,3},{3,0},{4,5},{5,6},{6,7},{7,4},{8,9},{9,10},{10,1... | collective-permute-start | bytes 12296 | tf_op jit(solution)/shard_map/ppermute | solution.py:281
  32.1 5.1 %collective-permute-start.1 = (f32[8,128]{1,0:T(8,128)S(1)}, f32[8,128]{1,0:T(8,128)S(1)}, u32[]{:S(2)}, u32[]{:S(2)}) collective-permute-start(f32[8,128]{1,0:T(8,128)S(1)} %get-tuple-element.15), channel_id=1, source_target_pairs={{0,2},{1,3},{2,0},{3,1},{4,6},{5,7},{6,4},{7,5},{8,10},{9,11},{10,... | collective-permute-start | bytes 12296 | tf_op jit(solution)/shard_map/ppermute | solution.py:281
  33.0 4.2 %collective-permute-start.2 = (f32[8,128]{1,0:T(8,128)S(1)}, f32[8,128]{1,0:T(8,128)S(1)}, u32[]{:S(2)}, u32[]{:S(2)}) collective-permute-start(f32[8,128]{1,0:T(8,128)S(1)} %get-tuple-element.15), channel_id=1, source_target_pairs={{0,3},{1,0},{2,1},{3,2},{4,7},{5,4},{6,5},{7,6},{8,11},{9,8},{10,9... | collective-permute-start | bytes 12296 | tf_op jit(solution)/shard_map/ppermute | solution.py:281
  37.2 1.1 copy-start
  38.9 61.7 %slice-start = ((s8[13107200]{0:T(1024)(128)(4,1)}), s8[4194304]{0:T(1024)(128)(4,1)S(1)}, s32[]{:S(2)}) async-start(s8[13107200]{0:T(1024)(128)(4,1)} %bitcast.8), calls=%async_computation.4 | async-start | bytes 8388608
  74.8 25.8 %slice-start.1 = ((s8[13107200]{0:T(1024)(128)(4,1)}), s8[4194304]{0:T(1024)(128)(4,1)S(1)}, s32[]{:S(2)}) async-start(s8[13107200]{0:T(1024)(128)(4,1)} %bitcast.8), calls=%async_computation.5 | async-start | bytes 8388608
  74.8 25.8 %slice-start.2 = ((s8[13107200]{0:T(1024)(128)(4,1)}), s8[4194304]{0:T(1024)(128)(4,1)S(1)}, s32[]{:S(2)}) async-start(s8[13107200]{0:T(1024)(128)(4,1)} %bitcast.8), calls=%async_computation.6 | async-start | bytes 8388608
  74.8 25.8 %slice-start.3 = ((s8[13107200]{0:T(1024)(128)(4,1)}), s8[524288]{0:T(1024)(128)(4,1)S(1)}, s32[]{:S(2)}) async-start(s8[13107200]{0:T(1024)(128)(4,1)} %bitcast.8), calls=%async_computation.7 | async-start | bytes 1048576

commit v3 on v2

--- a/solution.py
+++ b/solution.py
@@ -19,6 +19,10 @@
     return jnp.sum(column.T, axis=0, keepdims=True)
 
 
+def in_hbm(array):
+    return pltpu.with_memory_space_constraint(array, pltpu.HBM)
+
+
 def stream(x_ref, weights, sums, buffer, arrived, before):
     block = buffer.shape[1]
     blocks = weights[0].shape[0] // block
@@ -89,9 +93,9 @@
             pltpu.VMEM(tokens.shape, jnp.bfloat16),
             pltpu.SemaphoreType.DMA,
         ],
-        compiler_params=pltpu.CompilerParams(vmem_limit_bytes=53 << 20),
+        compiler_params=pltpu.CompilerParams(vmem_limit_bytes=24 << 20),
         name="project_value",
-    )(tokens, weight)
+    )(in_hbm(tokens), in_hbm(weight))
 
 
 def turn_tables(first_token, rows):
@@ -143,9 +147,9 @@
             pltpu.VMEM((AHEAD + 1, ROWS_IN, heads * HEAD_DIM), jnp.bfloat16),
             pltpu.SemaphoreType.DMA((AHEAD + 1,)),
         ],
-        compiler_params=pltpu.CompilerParams(vmem_limit_bytes=53 << 20),
+        compiler_params=pltpu.CompilerParams(vmem_limit_bytes=24 << 20),
         name="project_query_key",
-    )(flat, w_query, w_key)
+    )(flat, in_hbm(w_query), in_hbm(w_key))
 
 
 def pack(query, key, sums, gains, cosine, sine, slots, seqs):

time: 124 us -> 121 us (0.976)
  Pallas kernels: 28 us -> 25.9 us
    pallas_call x1, Pallas kernels: 11.6 us -> 9.53 us  [project_query_key(): pl.pallas_call(body, in_specs=[vmem, hbm, hbm], out_specs=[vmem] * 3, out...]
  transfers between devices with their start and end apart: 4 -> 4, of which waited for: 1 -> 2; matrix products, arithmetic and copies ran while one was open for 0% -> 0% of each run, Pallas kernels for 10% -> 9%
where the time goes in v3:
time: 121 us; the launch traced here: 119 us
  blocking collectives  73.3 us (61%)
  Pallas kernels  25.9 us (21%)
  starting transfers between devices  16.3 us (13%)
  waiting for transfers between devices  2.41 us (2%)
    all_to_all x3, blocking collectives, exchange(): return lax.all_to_all(array, axis, 0, 0, tiled=True)  73.3 us
    all_to_all x1, starting transfers between devices, exchange(): return lax.all_to_all(array, axis, 0, 0, tiled=True)  11.3 us
    pallas_call x1, Pallas kernels, project_query_key(): pl.pallas_call(body, in_specs=[vmem, hbm, hbm], out_specs=[vmem] * 3, out...  9.53 us
    pallas_call x1, Pallas kernels, project_value(): pl.pallas_call(body, in_specs=[pl.BlockSpec(memory_space=pltpu.HBM)] * 2,...  7.46 us
    ppermute x3, starting transfers between devices, local(): lax.ppermute(squares, 'tensor', [(i, (i + shift) % fold) for i in range(f...  5 us
    pallas_call x1, Pallas kernels, attend(): pl.pallas_call(body, out_shape=jax.ShapeDtypeStruct((blocks, rows, HEAD_D...  4.52 us
    pallas_call x1, Pallas kernels, project_out(): pl.pallas_call(body, in_specs=[vmem, vmem], out_specs=vmem, out_shape=jax...  3.66 us
  transfers between devices with their start and end apart: 4, of which 2 were waited for; matrix products, arithmetic and copies ran while one was open for 0% of the time, Pallas kernels for 9%

profile of v3, /device:TPU:8, one launch (start us, length us, event | category | flops | bytes accessed | tf_op | source)
XLA Modules:
  0.0 119.3 jit_solution(6748889680269684189)
XLA Ops:
  0.0 7.5 %project_value.1 = (bf16[128,5120]{1,0:T(8,128)(2,1)S(1)}, bf16[32,64,128]{2,1,0:T(8,128)(2,1)}) custom-call(bf16[64,2,5120]{2,1,0:T(2,128)(2,1)} %in_ref.1, bf16[5120,1280]{1,0:T(8,128)(2,1)} %w_ref.2), custom_call_target="tpu_custom_call" | custom-call | tf_op jit(solution)/shard_map/project_value/pallas_call | solution.py:80
  7.5 11.3 %all-to-all-start.1 = ((bf16[32,64,128]{2,1,0:T(8,128)(2,1)}), bf16[32,64,128]{2,1,0:T(8,128)(2,1)S(1)}, u32[]{:S(2)}, u32[]{:S(2)}) async-start(bf16[32,64,128]{2,1,0:T(8,128)(2,1)} %get-tuple-element.18), calls=%async_computation.1 | async-start | bytes 1048576 | tf_op jit(solution)/shard_map/all_to_all | solution.py:270
  18.8 0.0 copy-start
  18.8 0.0 copy-start.1
  18.8 9.5 %project_query_key.1 = (f32[10,128,128]{2,1,0:T(8,128)S(1)}, f32[10,128,128]{2,1,0:T(8,128)S(1)}, f32[8,128]{1,0:T(8,128)S(1)}) custom-call(bf16[128,5120]{1,0:T(8,128)(2,1)S(1)} %get-tuple-element.12.x_ref, bf16[5120,1280]{1,0:T(8,128)(2,1)} %wq_ref.1, bf16[5120,1280]{1,0:T(8,128)(2,1)} %wk_ref.1), custom_call_target="tpu_custom_call" | custom-call | tf_op jit(solution)/shard_map/project_query_key/pallas_call | solution.py:136
  28.4 1.7 %collective-permute-start = (f32[8,128]{1,0:T(8,128)S(1)}, f32[8,128]{1,0:T(8,128)S(1)}, u32[]{:S(2)}, u32[]{:S(2)}) collective-permute-start(f32[8,128]{1,0:T(8,128)S(1)} %get-tuple-element.15), channel_id=1, source_target_pairs={{0,1},{1,2},{2,3},{3,0},{4,5},{5,6},{6,7},{7,4},{8,9},{9,10},{10,1... | collective-permute-start | bytes 12296 | tf_op jit(solution)/shard_map/ppermute | solution.py:285
  30.0 0.9 collective-permute-start.1
  30.9 2.4 %collective-permute-start.2 = (f32[8,128]{1,0:T(8,128)S(1)}, f32[8,128]{1,0:T(8,128)S(1)}, u32[]{:S(2)}, u32[]{:S(2)}) collective-permute-start(f32[8,128]{1,0:T(8,128)S(1)} %get-tuple-element.15), channel_id=1, source_target_pairs={{0,3},{1,0},{2,1},{3,2},{4,7},{5,4},{6,5},{7,6},{8,11},{9,8},{10,9... | collective-permute-start | bytes 12296 | tf_op jit(solution)/shard_map/ppermute | solution.py:285
  33.4 0.0 copy-done
  33.4 0.0 copy-done.1
  33.4 0.1 turn_tables.1
  33.5 0.0 collective-permute-done
  33.6 1.6 %collective-permute-done.1 = f32[8,128]{1,0:T(8,128)S(1)} collective-permute-done((f32[8,128]{1,0:T(8,128)S(1)}, f32[8,128]{1,0:T(8,128)S(1)}, u32[]{:S(2)}, u32[]{:S(2)}) %collective-permute-start.1) | collective-permute-done | bytes 4128 | tf_op jit(solution)/shard_map/ppermute | solution.py:285
  35.1 0.0 collective-permute-done.2
  35.1 0.6 pack.1
  35.7 0.8 all-to-all-done.1.v_ref
  36.6 0.0 slice-start
  36.6 35.1 %all_to_all.20.in_ref = bf16[32,2,64,128]{3,2,1,0:T(8,128)(2,1)S(1)} all-to-all(bf16[32,2,64,128]{3,2,1,0:T(8,128)(2,1)S(1)} %pack.1), channel_id=1, replica_groups=mesh['dp'=2,'seq'=32,'tensor'=4] {'seq'}, dimensions={0} | all-to-all | bytes 2097152 | tf_op jit(solution)/shard_map/all_to_all | solution.py:270
  71.7 0.0 slice-start.1
  71.7 0.0 slice-start.2
  71.7 0.0 slice-start.3
  71.7 4.5 %attend.1 = bf16[32,64,128]{2,1,0:T(8,128)(2,1)S(1)} custom-call(bf16[32,2,64,128]{3,2,1,0:T(8,128)(2,1)S(1)} %all_to_all.20.in_ref, bf16[32,64,128]{2,1,0:T(8,128)(2,1)S(1)} %all-to-all-done.1.v_ref), custom_call_target="tpu_custom_call" | custom-call | flops 34359738368 | bytes 2097152 | tf_op jit(solution)/shard_map/attend/pallas_call | solution.py:217
  76.2 21.3 %all_to_all.21.in_ref = bf16[32,64,128]{2,1,0:T(8,128)(2,1)S(1)} all-to-all(bf16[32,64,128]{2,1,0:T(8,128)(2,1)S(1)} %attend.1), channel_id=1, replica_groups=mesh['dp'=2,'seq'=32,'tensor'=4] {'seq'}, dimensions={0} | all-to-all | bytes 1048576 | tf_op jit(solution)/shard_map/all_to_all | solution.py:270
  97.5 0.0 slice-done
  97.5 0.0 slice-done.1
  97.5 0.0 slice-done.2
  97.5 0.0 slice-done.3
  97.5 3.7 %project_out.1 = bf16[128,5120]{1,0:T(8,128)(2,1)S(1)} custom-call(bf16[32,64,128]{2,1,0:T(8,128)(2,1)S(1)} %all_to_all.21.in_ref, bf16[1280,5120]{1,0:T(8,128)(2,1)S(1)} %bitcast.9), custom_call_target="tpu_custom_call" | custom-call | flops 1677721600 | bytes 13107200 | tf_op jit(solution)/shard_map/project_out/pallas_call | solution.py:252
  101.2 16.9 %all_to_all.22 = bf16[4,32,5120]{2,1,0:T(8,128)(2,1)S(1)} all-to-all(bf16[4,32,5120]{2,1,0:T(8,128)(2,1)S(1)} %bitcast.10), channel_id=1, replica_groups=mesh['dp'=2,'seq'=32,'tensor'=4] {'tensor'}, dimensions={0} | all-to-all | bytes 2621440 | tf_op jit(solution)/shard_map/all_to_all | solution.py:270
  118.1 0.3 reduce_sum.12
  118.4 0.8 reshape.12
  (3 shorter events, 0.0 us)
Async XLA Ops:
  7.5 29.1 %all-to-all-start.1 = ((bf16[32,64,128]{2,1,0:T(8,128)(2,1)}), bf16[32,64,128]{2,1,0:T(8,128)(2,1)S(1)}, u32[]{:S(2)}, u32[]{:S(2)}) async-start(bf16[32,64,128]{2,1,0:T(8,128)(2,1)} %get-tuple-element.18), calls=%async_computation.1 | async-start | bytes 1048576 | tf_op jit(solution)/shard_map/all_to_all | solution.py:270
  18.8 14.6 %copy-start = (f32[1280]{0:T(1024)S(1)}, f32[1280]{0:T(1024)}, u32[]{:S(2)}) copy-start(f32[1280]{0:T(1024)} %param.13) | copy-start | bytes 15364
  18.8 14.6 %copy-start.1 = (f32[1280]{0:T(1024)S(1)}, f32[1280]{0:T(1024)}, u32[]{:S(2)}) copy-start(f32[1280]{0:T(1024)} %param.12) | copy-start | bytes 15364
  28.4 5.2 %collective-permute-start = (f32[8,128]{1,0:T(8,128)S(1)}, f32[8,128]{1,0:T(8,128)S(1)}, u32[]{:S(2)}, u32[]{:S(2)}) collective-permute-start(f32[8,128]{1,0:T(8,128)S(1)} %get-tuple-element.15), channel_id=1, source_target_pairs={{0,1},{1,2},{2,3},{3,0},{4,5},{5,6},{6,7},{7,4},{8,9},{9,10},{10,1... | collective-permute-start | bytes 12296 | tf_op jit(solution)/shard_map/ppermute | solution.py:285
  30.0 5.1 %collective-permute-start.1 = (f32[8,128]{1,0:T(8,128)S(1)}, f32[8,128]{1,0:T(8,128)S(1)}, u32[]{:S(2)}, u32[]{:S(2)}) collective-permute-start(f32[8,128]{1,0:T(8,128)S(1)} %get-tuple-element.15), channel_id=1, source_target_pairs={{0,2},{1,3},{2,0},{3,1},{4,6},{5,7},{6,4},{7,5},{8,10},{9,11},{10,... | collective-permute-start | bytes 12296 | tf_op jit(solution)/shard_map/ppermute | solution.py:285
  30.9 4.2 %collective-permute-start.2 = (f32[8,128]{1,0:T(8,128)S(1)}, f32[8,128]{1,0:T(8,128)S(1)}, u32[]{:S(2)}, u32[]{:S(2)}) collective-permute-start(f32[8,128]{1,0:T(8,128)S(1)} %get-tuple-element.15), channel_id=1, source_target_pairs={{0,3},{1,0},{2,1},{3,2},{4,7},{5,4},{6,5},{7,6},{8,11},{9,8},{10,9... | collective-permute-start | bytes 12296 | tf_op jit(solution)/shard_map/ppermute | solution.py:285
  36.6 60.9 %slice-start = ((s8[13107200]{0:T(1024)(128)(4,1)}), s8[4194304]{0:T(1024)(128)(4,1)S(1)}, s32[]{:S(2)}) async-start(s8[13107200]{0:T(1024)(128)(4,1)} %bitcast.8), calls=%async_computation.4 | async-start | bytes 8388608
  71.7 25.8 %slice-start.1 = ((s8[13107200]{0:T(1024)(128)(4,1)}), s8[4194304]{0:T(1024)(128)(4,1)S(1)}, s32[]{:S(2)}) async-start(s8[13107200]{0:T(1024)(128)(4,1)} %bitcast.8), calls=%async_computation.5 | async-start | bytes 8388608
  71.7 25.8 %slice-start.2 = ((s8[13107200]{0:T(1024)(128)(4,1)}), s8[4194304]{0:T(1024)(128)(4,1)S(1)}, s32[]{:S(2)}) async-start(s8[13107200]{0:T(1024)(128)(4,1)} %bitcast.8), calls=%async_computation.6 | async-start | bytes 8388608
  71.7 25.8 %slice-start.3 = ((s8[13107200]{0:T(1024)(128)(4,1)}), s8[524288]{0:T(1024)(128)(4,1)S(1)}, s32[]{:S(2)}) async-start(s8[13107200]{0:T(1024)(128)(4,1)} %bitcast.8), calls=%async_computation.7 | async-start | bytes 1048576

commit v4 on v3

--- a/solution.py
+++ b/solution.py
@@ -23,7 +23,7 @@
     return pltpu.with_memory_space_constraint(array, pltpu.HBM)
 
 
-def stream(x_ref, weights, sums, buffer, arrived, before):
+def stream(x_ref, weights, sums, buffer, arrived, before, beside):
     block = buffer.shape[1]
     blocks = weights[0].shape[0] // block
 
@@ -51,6 +51,7 @@
             columns = pl.ds(pl.multiple_of(n * block, block), block)
             part = buffer[(which * blocks + n) % (AHEAD + 1)]
             sums[which][...] += jnp.dot(x_ref[:, columns], part, preferred_element_type=jnp.float32)
+            beside(jnp.minimum(n + 1, blocks - 1))
             return 0
 
         sums[which][...] = jnp.zeros_like(sums[which])
@@ -66,11 +67,15 @@
         tokens_in = pltpu.make_async_copy(in_ref, token_ref, here)
         tokens_in.start()
 
+        def rows_of(n):
+            columns = pl.ds(pl.multiple_of(n * ROWS_IN, ROWS_IN), ROWS_IN)
+            x_ref[:, columns] = token_ref[:, :, columns].reshape(total, ROWS_IN)
+
         def before():
             tokens_in.wait()
-            x_ref[...] = token_ref[...].reshape(total, depth)
-
-        stream(x_ref, (w_ref,), (sums,), buffer, arrived, before)
+            rows_of(0)
+
+        stream(x_ref, (w_ref,), (sums,), buffer, arrived, before, rows_of)
         for h in range(heads):
             head_ref[h] = sums[:, h * HEAD_DIM : (h + 1) * HEAD_DIM]
             for j in range(seqs):
@@ -121,7 +126,7 @@
     heads = w_query.shape[1] // HEAD_DIM
 
     def body(x_ref, wq_ref, wk_ref, q_ref, k_ref, sums_ref, sums, buffer, arrived):
-        stream(x_ref, (wq_ref, wk_ref), (sums.at[0], sums.at[1]), buffer, arrived, lambda: None)
+        stream(x_ref, (wq_ref, wk_ref), (sums.at[0], sums.at[1]), buffer, arrived, lambda: None, lambda n: None)
         squares = []
         for which, out_ref in enumerate((q_ref, k_ref)):
             square = jnp.zeros((total, HEAD_DIM), jnp.float32)
@@ -189,35 +194,47 @@
     steps = blocks // per
     power = HEAD_DIM ** (-0.5) * LOG2E
 
-    def body(in_ref, v_ref, out_ref, s_ref):
+    def body(in_ref, v_ref, out_ref, s_ref, p_ref):
         row = lax.broadcasted_iota(jnp.int32, (BLOCK, BLOCK), 0)
         col = lax.broadcasted_iota(jnp.int32, (BLOCK, BLOCK), 1)
+
+        def score(i, c, top):
+            q = in_ref[per * i : per * (i + 1), 0].reshape(BLOCK, HEAD_DIM)
+            k = in_ref[per * c : per * (c + 1), 1].reshape(BLOCK, HEAD_DIM)
+            s = lax.dot_general(q, k, (((1,), (1,)), ((), ())), preferred_element_type=jnp.float32)
+            if c == i:
+                s = jnp.where(col <= row, s, -1e30)
+            s_ref[i % 2, :, c * BLOCK : (c + 1) * BLOCK] = s
+            best = jnp.maximum(s[:, :HEAD_DIM], s[:, HEAD_DIM:])
+            return best if top is None else jnp.maximum(top, best)
+
+        def weigh(i, c, top, total):
+            e = jnp.exp2((s_ref[i % 2, :, c * BLOCK : (c + 1) * BLOCK] - top) * power)
+            p_ref[i % 2, :, c * BLOCK : (c + 1) * BLOCK] = e.astype(jnp.bfloat16)
+            here = e[:, :HEAD_DIM] + e[:, HEAD_DIM:]
+            return here if total is None else total + here
+
+        top = score(0, 0, None)
         for i in range(steps):
-            q = in_ref[per * i : per * (i + 1), 0].reshape(BLOCK, HEAD_DIM)
-            top = None
-            for c in range(i + 1):
-                k = in_ref[per * c : per * (c + 1), 1].reshape(BLOCK, HEAD_DIM)
-                s = lax.dot_general(q, k, (((1,), (1,)), ((), ())), preferred_element_type=jnp.float32)
-                if c == i:
-                    s = jnp.where(col <= row, s, -1e30)
-                s_ref[:, c * BLOCK : (c + 1) * BLOCK] = s
-                best = jnp.maximum(s[:, :HEAD_DIM], s[:, HEAD_DIM:])
-                top = best if top is None else jnp.maximum(top, best)
-            top = jnp.max(top, axis=1, keepdims=True)
-            total = jnp.zeros((BLOCK, HEAD_DIM), jnp.float32)
-            acc = jnp.zeros((BLOCK, HEAD_DIM), jnp.float32)
-            for c in range(i + 1):
-                e = jnp.exp2((s_ref[:, c * BLOCK : (c + 1) * BLOCK] - top) * power)
-                total = total + e[:, :HEAD_DIM] + e[:, HEAD_DIM:]
-                v = v_ref[per * c : per * (c + 1)].reshape(BLOCK, HEAD_DIM)
-                acc = acc + jnp.dot(e.astype(jnp.bfloat16), v, preferred_element_type=jnp.float32)
+            best = jnp.max(top, axis=1, keepdims=True)
+            top, total = None, None
+            for c in range(i + 2):
+                if i + 1 < steps:
+                    top = score(i + 1, c, top)
+                if c <= i:
+                    total = weigh(i, c, best, total)
+            v = v_ref[: per * (i + 1)].reshape(BLOCK * (i + 1), HEAD_DIM)
+            acc = jnp.dot(p_ref[i % 2, :, : BLOCK * (i + 1)], v, preferred_element_type=jnp.float32)
             mixed = acc / jnp.sum(total, axis=1, keepdims=True)
             out_ref[per * i : per * (i + 1)] = mixed.astype(jnp.bfloat16).reshape(per, rows, HEAD_DIM)
 
     return pl.pallas_call(
         body,
         out_shape=jax.ShapeDtypeStruct((blocks, rows, HEAD_DIM), jnp.bfloat16),
-        scratch_shapes=[pltpu.VMEM((BLOCK, blocks * rows), jnp.float32)],
+        scratch_shapes=[
+            pltpu.VMEM((2, BLOCK, blocks * rows), jnp.float32),
+            pltpu.VMEM((2, BLOCK, blocks * rows), jnp.bfloat16),
+        ],
         compiler_params=pltpu.CompilerParams(vmem_limit_bytes=16 << 20),
         cost_estimate=pl.CostEstimate(
             flops=64 * (blocks * rows) ** 2 * HEAD_DIM,

time: 121 us -> 120 us (level)
  no operation moved by 1% of the time
where the time goes in v4:
time: 120 us; the launch traced here: 118 us
  blocking collectives  73.5 us (61%)
  Pallas kernels  24.7 us (21%)
  starting transfers between devices  16.3 us (14%)
  waiting for transfers between devices  2.41 us (2%)
    all_to_all x3, blocking collectives, exchange(): return lax.all_to_all(array, axis, 0, 0, tiled=True)  73.5 us
    all_to_all x1, starting transfers between devices, exchange(): return lax.all_to_all(array, axis, 0, 0, tiled=True)  11.3 us
    pallas_call x1, Pallas kernels, project_query_key(): pl.pallas_call(body, in_specs=[vmem, hbm, hbm], out_specs=[vmem] * 3, out...  9.55 us
    pallas_call x1, Pallas kernels, project_value(): pl.pallas_call(body, in_specs=[pl.BlockSpec(memory_space=pltpu.HBM)] * 2,...  7.35 us
    ppermute x3, starting transfers between devices, local(): lax.ppermute(squares, 'tensor', [(i, (i + shift) % fold) for i in range(f...  4.98 us
    pallas_call x1, Pallas kernels, project_out(): pl.pallas_call(body, in_specs=[vmem, vmem], out_specs=vmem, out_shape=jax...  3.66 us
    pallas_call x1, Pallas kernels, attend(): pl.pallas_call(body, out_shape=jax.ShapeDtypeStruct((blocks, rows, HEAD_D...  3.43 us
  transfers between devices with their start and end apart: 4, of which 2 were waited for; matrix products, arithmetic and copies ran while one was open for 0% of the time, Pallas kernels for 9%

profile of v4, /device:TPU:8, one launch (start us, length us, event | category | flops | bytes accessed | tf_op | source)
XLA Modules:
  0.0 118.2 jit_solution(10795103195476140307)
XLA Ops:
  0.0 7.3 %project_value.1 = (bf16[128,5120]{1,0:T(8,128)(2,1)S(1)}, bf16[32,64,128]{2,1,0:T(8,128)(2,1)}) custom-call(bf16[64,2,5120]{2,1,0:T(2,128)(2,1)} %in_ref.1, bf16[5120,1280]{1,0:T(8,128)(2,1)} %w_ref.2), custom_call_target="tpu_custom_call" | custom-call | tf_op jit(solution)/shard_map/project_value/pallas_call | solution.py:85
  7.4 11.3 %all-to-all-start.1 = ((bf16[32,64,128]{2,1,0:T(8,128)(2,1)}), bf16[32,64,128]{2,1,0:T(8,128)(2,1)S(1)}, u32[]{:S(2)}, u32[]{:S(2)}) async-start(bf16[32,64,128]{2,1,0:T(8,128)(2,1)} %get-tuple-element.18), calls=%async_computation.1 | async-start | bytes 1048576 | tf_op jit(solution)/shard_map/all_to_all | solution.py:287
  18.7 0.0 copy-start
  18.7 0.0 copy-start.1
  18.7 9.5 %project_query_key.1 = (f32[10,128,128]{2,1,0:T(8,128)S(1)}, f32[10,128,128]{2,1,0:T(8,128)S(1)}, f32[8,128]{1,0:T(8,128)S(1)}) custom-call(bf16[128,5120]{1,0:T(8,128)(2,1)S(1)} %get-tuple-element.12.x_ref, bf16[5120,1280]{1,0:T(8,128)(2,1)} %wq_ref.1, bf16[5120,1280]{1,0:T(8,128)(2,1)} %wk_ref.1), custom_call_target="tpu_custom_call" | custom-call | tf_op jit(solution)/shard_map/project_query_key/pallas_call | solution.py:141
  28.3 1.6 %collective-permute-start = (f32[8,128]{1,0:T(8,128)S(1)}, f32[8,128]{1,0:T(8,128)S(1)}, u32[]{:S(2)}, u32[]{:S(2)}) collective-permute-start(f32[8,128]{1,0:T(8,128)S(1)} %get-tuple-element.15), channel_id=1, source_target_pairs={{0,1},{1,2},{2,3},{3,0},{4,5},{5,6},{6,7},{7,4},{8,9},{9,10},{10,1... | collective-permute-start | bytes 12296 | tf_op jit(solution)/shard_map/ppermute | solution.py:302
  29.9 1.0 collective-permute-start.1
  30.9 2.4 %collective-permute-start.2 = (f32[8,128]{1,0:T(8,128)S(1)}, f32[8,128]{1,0:T(8,128)S(1)}, u32[]{:S(2)}, u32[]{:S(2)}) collective-permute-start(f32[8,128]{1,0:T(8,128)S(1)} %get-tuple-element.15), channel_id=1, source_target_pairs={{0,3},{1,0},{2,1},{3,2},{4,7},{5,4},{6,5},{7,6},{8,11},{9,8},{10,9... | collective-permute-start | bytes 12296 | tf_op jit(solution)/shard_map/ppermute | solution.py:302
  33.3 0.0 copy-done
  33.3 0.0 copy-done.1
  33.3 0.1 turn_tables.1
  33.4 0.0 collective-permute-done
  33.4 1.6 %collective-permute-done.1 = f32[8,128]{1,0:T(8,128)S(1)} collective-permute-done((f32[8,128]{1,0:T(8,128)S(1)}, f32[8,128]{1,0:T(8,128)S(1)}, u32[]{:S(2)}, u32[]{:S(2)}) %collective-permute-start.1) | collective-permute-done | bytes 4128 | tf_op jit(solution)/shard_map/ppermute | solution.py:302
  35.0 0.0 collective-permute-done.2
  35.0 0.6 pack.1
  35.6 0.8 all-to-all-done.1.v_ref
  36.5 0.0 slice-start
  36.5 35.1 %all_to_all.20.in_ref = bf16[32,2,64,128]{3,2,1,0:T(8,128)(2,1)S(1)} all-to-all(bf16[32,2,64,128]{3,2,1,0:T(8,128)(2,1)S(1)} %pack.1), channel_id=1, replica_groups=mesh['dp'=2,'seq'=32,'tensor'=4] {'seq'}, dimensions={0} | all-to-all | bytes 2097152 | tf_op jit(solution)/shard_map/all_to_all | solution.py:287
  71.6 0.0 slice-start.1
  71.6 0.0 slice-start.2
  71.6 0.0 slice-start.3
  71.6 3.4 %attend.1 = bf16[32,64,128]{2,1,0:T(8,128)(2,1)S(1)} custom-call(bf16[32,2,64,128]{3,2,1,0:T(8,128)(2,1)S(1)} %all_to_all.20.in_ref, bf16[32,64,128]{2,1,0:T(8,128)(2,1)S(1)} %all-to-all-done.1.v_ref), custom_call_target="tpu_custom_call" | custom-call | flops 34359738368 | bytes 2097152 | tf_op jit(solution)/shard_map/attend/pallas_call | solution.py:231
  75.0 21.3 %all_to_all.21.in_ref = bf16[32,64,128]{2,1,0:T(8,128)(2,1)S(1)} all-to-all(bf16[32,64,128]{2,1,0:T(8,128)(2,1)S(1)} %attend.1), channel_id=1, replica_groups=mesh['dp'=2,'seq'=32,'tensor'=4] {'seq'}, dimensions={0} | all-to-all | bytes 1048576 | tf_op jit(solution)/shard_map/all_to_all | solution.py:287
  96.3 0.0 slice-done
  96.3 0.0 slice-done.1
  96.3 0.0 slice-done.2
  96.3 0.0 slice-done.3
  96.3 3.7 %project_out.1 = bf16[128,5120]{1,0:T(8,128)(2,1)S(1)} custom-call(bf16[32,64,128]{2,1,0:T(8,128)(2,1)S(1)} %all_to_all.21.in_ref, bf16[1280,5120]{1,0:T(8,128)(2,1)S(1)} %bitcast.9), custom_call_target="tpu_custom_call" | custom-call | flops 1677721600 | bytes 13107200 | tf_op jit(solution)/shard_map/project_out/pallas_call | solution.py:269
  100.0 17.1 %all_to_all.22 = bf16[4,32,5120]{2,1,0:T(8,128)(2,1)S(1)} all-to-all(bf16[4,32,5120]{2,1,0:T(8,128)(2,1)S(1)} %bitcast.10), channel_id=1, replica_groups=mesh['dp'=2,'seq'=32,'tensor'=4] {'tensor'}, dimensions={0} | all-to-all | bytes 2621440 | tf_op jit(solution)/shard_map/all_to_all | solution.py:287
  117.1 0.3 reduce_sum.12
  117.4 0.8 reshape.12
  (3 shorter events, 0.0 us)
Async XLA Ops:
  7.4 29.1 %all-to-all-start.1 = ((bf16[32,64,128]{2,1,0:T(8,128)(2,1)}), bf16[32,64,128]{2,1,0:T(8,128)(2,1)S(1)}, u32[]{:S(2)}, u32[]{:S(2)}) async-start(bf16[32,64,128]{2,1,0:T(8,128)(2,1)} %get-tuple-element.18), calls=%async_computation.1 | async-start | bytes 1048576 | tf_op jit(solution)/shard_map/all_to_all | solution.py:287
  18.7 14.6 %copy-start = (f32[1280]{0:T(1024)S(1)}, f32[1280]{0:T(1024)}, u32[]{:S(2)}) copy-start(f32[1280]{0:T(1024)} %param.13) | copy-start | bytes 15364
  18.7 14.6 %copy-start.1 = (f32[1280]{0:T(1024)S(1)}, f32[1280]{0:T(1024)}, u32[]{:S(2)}) copy-start(f32[1280]{0:T(1024)} %param.12) | copy-start | bytes 15364
  28.3 5.2 %collective-permute-start = (f32[8,128]{1,0:T(8,128)S(1)}, f32[8,128]{1,0:T(8,128)S(1)}, u32[]{:S(2)}, u32[]{:S(2)}) collective-permute-start(f32[8,128]{1,0:T(8,128)S(1)} %get-tuple-element.15), channel_id=1, source_target_pairs={{0,1},{1,2},{2,3},{3,0},{4,5},{5,6},{6,7},{7,4},{8,9},{9,10},{10,1... | collective-permute-start | bytes 12296 | tf_op jit(solution)/shard_map/ppermute | solution.py:302
  29.9 5.1 %collective-permute-start.1 = (f32[8,128]{1,0:T(8,128)S(1)}, f32[8,128]{1,0:T(8,128)S(1)}, u32[]{:S(2)}, u32[]{:S(2)}) collective-permute-start(f32[8,128]{1,0:T(8,128)S(1)} %get-tuple-element.15), channel_id=1, source_target_pairs={{0,2},{1,3},{2,0},{3,1},{4,6},{5,7},{6,4},{7,5},{8,10},{9,11},{10,... | collective-permute-start | bytes 12296 | tf_op jit(solution)/shard_map/ppermute | solution.py:302
  30.9 4.2 %collective-permute-start.2 = (f32[8,128]{1,0:T(8,128)S(1)}, f32[8,128]{1,0:T(8,128)S(1)}, u32[]{:S(2)}, u32[]{:S(2)}) collective-permute-start(f32[8,128]{1,0:T(8,128)S(1)} %get-tuple-element.15), channel_id=1, source_target_pairs={{0,3},{1,0},{2,1},{3,2},{4,7},{5,4},{6,5},{7,6},{8,11},{9,8},{10,9... | collective-permute-start | bytes 12296 | tf_op jit(solution)/shard_map/ppermute | solution.py:302
  36.5 59.9 %slice-start = ((s8[13107200]{0:T(1024)(128)(4,1)}), s8[4194304]{0:T(1024)(128)(4,1)S(1)}, s32[]{:S(2)}) async-start(s8[13107200]{0:T(1024)(128)(4,1)} %bitcast.8), calls=%async_computation.4 | async-start | bytes 8388608
  71.6 24.7 %slice-start.1 = ((s8[13107200]{0:T(1024)(128)(4,1)}), s8[4194304]{0:T(1024)(128)(4,1)S(1)}, s32[]{:S(2)}) async-start(s8[13107200]{0:T(1024)(128)(4,1)} %bitcast.8), calls=%async_computation.5 | async-start | bytes 8388608
  71.6 24.7 %slice-start.2 = ((s8[13107200]{0:T(1024)(128)(4,1)}), s8[4194304]{0:T(1024)(128)(4,1)S(1)}, s32[]{:S(2)}) async-start(s8[13107200]{0:T(1024)(128)(4,1)} %bitcast.8), calls=%async_computation.6 | async-start | bytes 8388608
  71.6 24.7 %slice-start.3 = ((s8[13107200]{0:T(1024)(128)(4,1)}), s8[524288]{0:T(1024)(128)(4,1)S(1)}, s32[]{:S(2)}) async-start(s8[13107200]{0:T(1024)(128)(4,1)} %bitcast.8), calls=%async_computation.7 | async-start | bytes 1048576

commit v5 on v4

--- a/solution.py
+++ b/solution.py
@@ -283,6 +283,23 @@
     )(parts, weight)
 
 
+def add_up(pieces, seqs):
+    count, total, depth = pieces.shape
+
+    def body(in_ref, out_ref):
+        whole = in_ref[0].astype(jnp.float32)
+        for other in range(1, count):
+            whole = whole + in_ref[other].astype(jnp.float32)
+        out_ref[...] = whole.astype(jnp.bfloat16).reshape(total // seqs, seqs, depth)
+
+    return pl.pallas_call(
+        body,
+        out_shape=jax.ShapeDtypeStruct((total // seqs, seqs, depth), jnp.bfloat16),
+        compiler_params=pltpu.CompilerParams(vmem_limit_bytes=8 << 20),
+        name="add_up",
+    )(pieces)
+
+
 def exchange(array, axis):
     return lax.all_to_all(array, axis, 0, 0, tiled=True)
 
@@ -306,8 +323,7 @@
     mixed = exchange(attend(exchange(sent_qk, "seq"), got_v), "seq")
     partial = project_out(mixed, w_out, seqs)
     pieces = exchange(partial.reshape(fold, -1, depth), "tensor")
-    attended = jnp.sum(pieces.astype(jnp.float32), axis=0).astype(jnp.bfloat16)
-    return attended.reshape(-1, seqs, depth)
+    return add_up(pieces, seqs)
 
 
 def solution(mesh):

time: 120 us -> 120 us (level)
  no operation moved by 1% of the time
where the time goes in v5:
time: 120 us; the launch traced here: 118 us
  blocking collectives  73.8 us (62%)
  Pallas kernels  25.7 us (21%)
  starting transfers between devices  16.3 us (14%)
  waiting for transfers between devices  2.42 us (2%)
    all_to_all x3, blocking collectives, exchange(): return lax.all_to_all(array, axis, 0, 0, tiled=True)  73.8 us
    all_to_all x1, starting transfers between devices, exchange(): return lax.all_to_all(array, axis, 0, 0, tiled=True)  11.3 us
    pallas_call x1, Pallas kernels, project_query_key(): pl.pallas_call(body, in_specs=[vmem, hbm, hbm], out_specs=[vmem] * 3, out...  9.55 us
    pallas_call x1, Pallas kernels, project_value(): pl.pallas_call(body, in_specs=[pl.BlockSpec(memory_space=pltpu.HBM)] * 2,...  7.35 us
    ppermute x3, starting transfers between devices, local(): lax.ppermute(squares, 'tensor', [(i, (i + shift) % fold) for i in range(f...  4.97 us
    pallas_call x1, Pallas kernels, project_out(): pl.pallas_call(body, in_specs=[vmem, vmem], out_specs=vmem, out_shape=jax...  3.66 us
    pallas_call x1, Pallas kernels, attend(): pl.pallas_call(body, out_shape=jax.ShapeDtypeStruct((blocks, rows, HEAD_D...  3.43 us
  transfers between devices with their start and end apart: 4, of which 2 were waited for; matrix products, arithmetic and copies ran while one was open for 0% of the time, Pallas kernels for 9%

profile of v5, /device:TPU:8, one launch (start us, length us, event | category | flops | bytes accessed | tf_op | source)
XLA Modules:
  0.0 118.3 jit_solution(2376975849151266607)
XLA Ops:
  0.0 7.3 %project_value.1 = (bf16[128,5120]{1,0:T(8,128)(2,1)S(1)}, bf16[32,64,128]{2,1,0:T(8,128)(2,1)}) custom-call(bf16[64,2,5120]{2,1,0:T(2,128)(2,1)} %in_ref.1, bf16[5120,1280]{1,0:T(8,128)(2,1)} %w_ref.2), custom_call_target="tpu_custom_call" | custom-call | tf_op jit(solution)/shard_map/project_value/pallas_call | solution.py:85
  7.4 11.3 %all-to-all-start.1 = ((bf16[32,64,128]{2,1,0:T(8,128)(2,1)}), bf16[32,64,128]{2,1,0:T(8,128)(2,1)S(1)}, u32[]{:S(2)}, u32[]{:S(2)}) async-start(bf16[32,64,128]{2,1,0:T(8,128)(2,1)} %get-tuple-element.18), calls=%async_computation.1 | async-start | bytes 1048576 | tf_op jit(solution)/shard_map/all_to_all | solution.py:304
  18.7 0.0 copy-start
  18.7 0.0 copy-start.1
  18.7 9.5 %project_query_key.1 = (f32[10,128,128]{2,1,0:T(8,128)S(1)}, f32[10,128,128]{2,1,0:T(8,128)S(1)}, f32[8,128]{1,0:T(8,128)S(1)}) custom-call(bf16[128,5120]{1,0:T(8,128)(2,1)S(1)} %get-tuple-element.12.x_ref, bf16[5120,1280]{1,0:T(8,128)(2,1)} %wq_ref.1, bf16[5120,1280]{1,0:T(8,128)(2,1)} %wk_ref.1), custom_call_target="tpu_custom_call" | custom-call | tf_op jit(solution)/shard_map/project_query_key/pallas_call | solution.py:141
  28.3 1.6 %collective-permute-start = (f32[8,128]{1,0:T(8,128)S(1)}, f32[8,128]{1,0:T(8,128)S(1)}, u32[]{:S(2)}, u32[]{:S(2)}) collective-permute-start(f32[8,128]{1,0:T(8,128)S(1)} %get-tuple-element.15), channel_id=1, source_target_pairs={{0,1},{1,2},{2,3},{3,0},{4,5},{5,6},{6,7},{7,4},{8,9},{9,10},{10,1... | collective-permute-start | bytes 12296 | tf_op jit(solution)/shard_map/ppermute | solution.py:319
  29.9 1.0 collective-permute-start.1
  30.9 2.4 %collective-permute-start.2 = (f32[8,128]{1,0:T(8,128)S(1)}, f32[8,128]{1,0:T(8,128)S(1)}, u32[]{:S(2)}, u32[]{:S(2)}) collective-permute-start(f32[8,128]{1,0:T(8,128)S(1)} %get-tuple-element.15), channel_id=1, source_target_pairs={{0,3},{1,0},{2,1},{3,2},{4,7},{5,4},{6,5},{7,6},{8,11},{9,8},{10,9... | collective-permute-start | bytes 12296 | tf_op jit(solution)/shard_map/ppermute | solution.py:319
  33.2 0.0 copy-done
  33.2 0.0 copy-done.1
  33.3 0.1 turn_tables.1
  33.4 0.0 collective-permute-done
  33.4 1.6 %collective-permute-done.1 = f32[8,128]{1,0:T(8,128)S(1)} collective-permute-done((f32[8,128]{1,0:T(8,128)S(1)}, f32[8,128]{1,0:T(8,128)S(1)}, u32[]{:S(2)}, u32[]{:S(2)}) %collective-permute-start.1) | collective-permute-done | bytes 4128 | tf_op jit(solution)/shard_map/ppermute | solution.py:319
  35.0 0.0 collective-permute-done.2
  35.0 0.6 pack.1
  35.6 0.8 all-to-all-done.1.v_ref
  36.5 0.0 slice-start
  36.5 35.1 %all_to_all.20.in_ref = bf16[32,2,64,128]{3,2,1,0:T(8,128)(2,1)S(1)} all-to-all(bf16[32,2,64,128]{3,2,1,0:T(8,128)(2,1)S(1)} %pack.1), channel_id=1, replica_groups=mesh['dp'=2,'seq'=32,'tensor'=4] {'seq'}, dimensions={0} | all-to-all | bytes 2097152 | tf_op jit(solution)/shard_map/all_to_all | solution.py:304
  71.6 0.0 slice-start.1
  71.6 0.0 slice-start.2
  71.6 0.0 slice-start.3
  71.6 3.4 %attend.1 = bf16[32,64,128]{2,1,0:T(8,128)(2,1)S(1)} custom-call(bf16[32,2,64,128]{3,2,1,0:T(8,128)(2,1)S(1)} %all_to_all.20.in_ref, bf16[32,64,128]{2,1,0:T(8,128)(2,1)S(1)} %all-to-all-done.1.v_ref), custom_call_target="tpu_custom_call" | custom-call | flops 34359738368 | bytes 2097152 | tf_op jit(solution)/shard_map/attend/pallas_call | solution.py:231
  75.0 21.3 %all_to_all.21.in_ref = bf16[32,64,128]{2,1,0:T(8,128)(2,1)S(1)} all-to-all(bf16[32,64,128]{2,1,0:T(8,128)(2,1)S(1)} %attend.1), channel_id=1, replica_groups=mesh['dp'=2,'seq'=32,'tensor'=4] {'seq'}, dimensions={0} | all-to-all | bytes 1048576 | tf_op jit(solution)/shard_map/all_to_all | solution.py:304
  96.3 0.0 slice-done
  96.3 0.0 slice-done.1
  96.3 0.0 slice-done.2
  96.3 0.0 slice-done.3
  96.4 3.7 %project_out.1 = bf16[128,5120]{1,0:T(8,128)(2,1)S(1)} custom-call(bf16[32,64,128]{2,1,0:T(8,128)(2,1)S(1)} %all_to_all.21.in_ref, bf16[1280,5120]{1,0:T(8,128)(2,1)S(1)} %bitcast.9), custom_call_target="tpu_custom_call" | custom-call | flops 1677721600 | bytes 13107200 | tf_op jit(solution)/shard_map/project_out/pallas_call | solution.py:269
  100.0 17.4 %all_to_all.22.in_ref = bf16[4,32,5120]{2,1,0:T(8,128)(2,1)S(1)} all-to-all(bf16[4,32,5120]{2,1,0:T(8,128)(2,1)S(1)} %bitcast.10), channel_id=1, replica_groups=mesh['dp'=2,'seq'=32,'tensor'=4] {'tensor'}, dimensions={0} | all-to-all | bytes 2621440 | tf_op jit(solution)/shard_map/all_to_all | solution.py:304
  117.4 0.9 add_up.1
  (3 shorter events, 0.0 us)
Async XLA Ops:
  7.4 29.1 %all-to-all-start.1 = ((bf16[32,64,128]{2,1,0:T(8,128)(2,1)}), bf16[32,64,128]{2,1,0:T(8,128)(2,1)S(1)}, u32[]{:S(2)}, u32[]{:S(2)}) async-start(bf16[32,64,128]{2,1,0:T(8,128)(2,1)} %get-tuple-element.18), calls=%async_computation.1 | async-start | bytes 1048576 | tf_op jit(solution)/shard_map/all_to_all | solution.py:304
  18.7 14.5 %copy-start = (f32[1280]{0:T(1024)S(1)}, f32[1280]{0:T(1024)}, u32[]{:S(2)}) copy-start(f32[1280]{0:T(1024)} %param.13) | copy-start | bytes 15364
  18.7 14.5 %copy-start.1 = (f32[1280]{0:T(1024)S(1)}, f32[1280]{0:T(1024)}, u32[]{:S(2)}) copy-start(f32[1280]{0:T(1024)} %param.12) | copy-start | bytes 15364
  28.3 5.1 %collective-permute-start = (f32[8,128]{1,0:T(8,128)S(1)}, f32[8,128]{1,0:T(8,128)S(1)}, u32[]{:S(2)}, u32[]{:S(2)}) collective-permute-start(f32[8,128]{1,0:T(8,128)S(1)} %get-tuple-element.15), channel_id=1, source_target_pairs={{0,1},{1,2},{2,3},{3,0},{4,5},{5,6},{6,7},{7,4},{8,9},{9,10},{10,1... | collective-permute-start | bytes 12296 | tf_op jit(solution)/shard_map/ppermute | solution.py:319
  29.9 5.1 %collective-permute-start.1 = (f32[8,128]{1,0:T(8,128)S(1)}, f32[8,128]{1,0:T(8,128)S(1)}, u32[]{:S(2)}, u32[]{:S(2)}) collective-permute-start(f32[8,128]{1,0:T(8,128)S(1)} %get-tuple-element.15), channel_id=1, source_target_pairs={{0,2},{1,3},{2,0},{3,1},{4,6},{5,7},{6,4},{7,5},{8,10},{9,11},{10,... | collective-permute-start | bytes 12296 | tf_op jit(solution)/shard_map/ppermute | solution.py:319
  30.9 4.1 %collective-permute-start.2 = (f32[8,128]{1,0:T(8,128)S(1)}, f32[8,128]{1,0:T(8,128)S(1)}, u32[]{:S(2)}, u32[]{:S(2)}) collective-permute-start(f32[8,128]{1,0:T(8,128)S(1)} %get-tuple-element.15), channel_id=1, source_target_pairs={{0,3},{1,0},{2,1},{3,2},{4,7},{5,4},{6,5},{7,6},{8,11},{9,8},{10,9... | collective-permute-start | bytes 12296 | tf_op jit(solution)/shard_map/ppermute | solution.py:319
  36.5 59.9 %slice-start = ((s8[13107200]{0:T(1024)(128)(4,1)}), s8[4194304]{0:T(1024)(128)(4,1)S(1)}, s32[]{:S(2)}) async-start(s8[13107200]{0:T(1024)(128)(4,1)} %bitcast.8), calls=%async_computation.4 | async-start | bytes 8388608
  71.6 24.8 %slice-start.1 = ((s8[13107200]{0:T(1024)(128)(4,1)}), s8[4194304]{0:T(1024)(128)(4,1)S(1)}, s32[]{:S(2)}) async-start(s8[13107200]{0:T(1024)(128)(4,1)} %bitcast.8), calls=%async_computation.5 | async-start | bytes 8388608
  71.6 24.8 %slice-start.2 = ((s8[13107200]{0:T(1024)(128)(4,1)}), s8[4194304]{0:T(1024)(128)(4,1)S(1)}, s32[]{:S(2)}) async-start(s8[13107200]{0:T(1024)(128)(4,1)} %bitcast.8), calls=%async_computation.6 | async-start | bytes 8388608
  71.6 24.8 %slice-start.3 = ((s8[13107200]{0:T(1024)(128)(4,1)}), s8[524288]{0:T(1024)(128)(4,1)S(1)}, s32[]{:S(2)}) async-start(s8[13107200]{0:T(1024)(128)(4,1)} %bitcast.8), calls=%async_computation.7 | async-start | bytes 1048576
